TPU v7x, 16 devices: a 4x2x1 block of a 4x4x8 slice. The times are simulated.
16 devices in a mesh: replica: 2 (over y, z), stage: 8 (over x, core).
Axes of the slice: x: 4, y: 2, z: 1, core: 2. Of those that a mesh axis runs over, the one named last changes fastest.
The devices are a block of a 4x4x8 slice.
Arguments:
- x_dec: bfloat16 [8, 32, 896], P('replica'), parts along dimension 0
- x_pre: bfloat16 [8, 32, 896], P('replica'), parts along dimension 0
- dec_len: int32 [8, 32], P('replica'), parts along dimension 0
- pre_len: int32 [2], P('replica'), parts along dimension 0
- g_attn: bfloat16 [8, 896], P('stage')
- w_q: bfloat16 [8, 896, 896], P('stage')
- w_k: bfloat16 [8, 896, 128], P('stage')
- w_v: bfloat16 [8, 896, 128], P('stage')
- w_o: bfloat16 [8, 896, 896], P('stage')
- g_mlp: bfloat16 [8, 896], P('stage')
- w_gate: bfloat16 [8, 896, 4864], P('stage')
- w_up: bfloat16 [8, 896, 4864], P('stage')
- w_down: bfloat16 [8, 4864, 896], P('stage')
- g_final: bfloat16 [896], replicated
- w_head: bfloat16 [896, 8192], replicated
- k_dec: bfloat16 [8, 8, 32, 256, 2, 64], P('stage', 'replica'), parts along dimension 1
- v_dec: bfloat16 [8, 8, 32, 256, 2, 64], P('stage', 'replica'), parts along dimension 1
- k_pre: bfloat16 [8, 512, 2, 64], P('stage', 'replica'), parts along dimension 1
- v_pre: bfloat16 [8, 512, 2, 64], P('stage', 'replica'), parts along dimension 1
Outputs:
- output 1: float32 [8, 33, 8192], P('replica'), parts along dimension 0
- output 2: bfloat16 [8, 8, 32, 256, 2, 64], P('stage', 'replica'), parts along dimension 1
- output 3: bfloat16 [8, 8, 32, 256, 2, 64], P('stage', 'replica'), parts along dimension 1
- output 4: bfloat16 [8, 512, 2, 64], P('stage', 'replica'), parts along dimension 1
- output 5: bfloat16 [8, 512, 2, 64], P('stage', 'replica'), parts along dimension 1
There are 2 independent parts. A program takes and returns all parts, laid end to end along the dimension named above; an argument that names none is the same for every part.
All inputs are finite; a program needn't handle non-finite values.
Results may differ from a plain program's by a relative error of at most 0.02.
Values are sent between devices in bfloat16 or wider.
A program may use at most 768 MiB of HBM per device.

v0:
```python
import jax
import jax.numpy as jnp
from jax import lax
from jax.sharding import PartitionSpec as P

NORM_EPS = 1e-6
ROPE_BASE = 10000.0


def rms_norm(acts, gain):
    acts_f = acts.astype(jnp.float32)
    inv_rms = lax.rsqrt(jnp.mean(acts_f * acts_f, axis=-1, keepdims=True) + NORM_EPS)
    return (acts_f * inv_rms * gain.astype(jnp.float32)).astype(jnp.bfloat16)


def rotate(proj, positions):
    head_dim = proj.shape[-1]
    half_dim = head_dim // 2
    inv_freq = ROPE_BASE ** (-jnp.arange(half_dim, dtype=jnp.float32) * (2.0 / head_dim))
    angles = positions.astype(jnp.float32)[:, None, None] * inv_freq
    cosine = jnp.cos(angles)
    sine_v = jnp.sin(angles)
    first_h = proj[..., :half_dim]
    second_h = proj[..., half_dim:]
    return jnp.concatenate([first_h * cosine - second_h * sine_v, second_h * cosine + first_h * sine_v], axis=-1)


def project(normed, positions, wq_l, wk_l, wv_l, kv_count, head_dim):
    n_rows = normed.shape[0]
    q_heads = wq_l.shape[1] // head_dim
    q_proj = jnp.dot(normed, wq_l, preferred_element_type=jnp.float32).reshape(n_rows, q_heads, head_dim)
    k_proj = jnp.dot(normed, wk_l, preferred_element_type=jnp.float32).reshape(n_rows, kv_count, head_dim)
    q_grp = rotate(q_proj, positions).astype(jnp.bfloat16).reshape(n_rows, kv_count, q_heads // kv_count, head_dim)
    k_new = rotate(k_proj, positions).astype(jnp.bfloat16)
    v_new = jnp.dot(normed, wv_l, preferred_element_type=jnp.float32).astype(jnp.bfloat16).reshape(n_rows, kv_count, head_dim)
    return q_grp, k_new, v_new


def attend(q_grp, keys_in, values_in, valid, score_form, mix_form):
    att_scale = q_grp.shape[-1] ** -0.5
    scores = jnp.einsum(score_form, q_grp, keys_in, preferred_element_type=jnp.float32) * att_scale
    probs = jax.nn.softmax(jnp.where(valid, scores, -1e30), axis=-1).astype(jnp.bfloat16)
    mixed = jnp.einsum(mix_form, probs, values_in, preferred_element_type=jnp.float32)
    return mixed.astype(jnp.bfloat16).reshape(q_grp.shape[0], -1)


def finish(acts, attn_out, wo_l, g_ffn, wg_l, wu_l, wd_l):
    acts = (acts.astype(jnp.float32) + jnp.dot(attn_out, wo_l, preferred_element_type=jnp.float32)).astype(jnp.bfloat16)
    normed = rms_norm(acts, g_ffn)
    gate_f = jnp.dot(normed, wg_l, preferred_element_type=jnp.float32)
    up_proj = jnp.dot(normed, wu_l, preferred_element_type=jnp.float32)
    hidden_act = (jax.nn.silu(gate_f) * up_proj).astype(jnp.bfloat16)
    return (acts.astype(jnp.float32) + jnp.dot(hidden_act, wd_l, preferred_element_type=jnp.float32)).astype(jnp.bfloat16)


def run_stages(src_rows, n_keep, keep_fn, stage_fn, caches, fwd_perm):
    n_micro, n_rows, hidden = src_rows.shape
    stage_idx = lax.axis_index('stage')
    n_ticks = n_micro + len(fwd_perm)

    def tick_fn(tick_idx, loop_carry):
        in_rows, collect, cache_state = loop_carry
        micro_idx = tick_idx - stage_idx
        active = (micro_idx >= 0) & (micro_idx < n_micro)
        micro_c = jnp.clip(micro_idx, 0, n_micro - 1)

        def compute(carry_in):
            rows_in, collect_in, caches_in = carry_in
            first_in = lax.dynamic_index_in_dim(src_rows, micro_c, 0, keepdims=False)
            acts = jnp.where(stage_idx == 0, first_in, rows_in)
            acts, caches_out = stage_fn(acts, micro_c, caches_in)
            collect_out = lax.dynamic_update_slice(collect_in, keep_fn(acts)[None], (micro_c, 0, 0))
            return acts, collect_out, caches_out

        sent_rows, collect, cache_state = lax.cond(active, compute, lambda carry_in: carry_in, (in_rows, collect, cache_state))
        return lax.ppermute(sent_rows, 'stage', fwd_perm), collect, cache_state

    init_carry = (jnp.zeros((n_rows, hidden), src_rows.dtype), jnp.zeros((n_micro, n_keep, hidden), src_rows.dtype), caches)
    last_carry = lax.fori_loop(0, n_ticks, tick_fn, init_carry)
    return last_carry[1], last_carry[2]


def solution(mesh):
    n_stages = mesh.shape['stage']
    fwd_perm = [(src_idx, src_idx + 1) for src_idx in range(n_stages - 1)]
    part_spec = P('replica')
    layer_spec = P('stage')
    cache_spec = P('stage', 'replica')
    in_specs = (part_spec,) * 4 + (layer_spec,) * 9 + (P(), P()) + (cache_spec,) * 4
    out_specs = (part_spec,) + (cache_spec,) * 4

    def device_fn(x_dec, x_pre, dec_len, pre_len, g_attn, w_q, w_k, w_v, w_o, g_mlp, w_gate, w_up, w_down, g_final, w_head, k_dec, v_dec, k_pre, v_pre):
        n_micro, dec_rows, hidden = x_dec.shape
        seg_len = x_pre.shape[1]
        local_layers, cache_len, kv_count, head_dim = k_pre.shape
        stage_idx = lax.axis_index('stage')
        cache_pos = jnp.arange(cache_len)

        def stage_fn(acts, micro_c, caches):
            kd_all, vd_all, kp_all, vp_all = caches
            dec_pos = lax.dynamic_index_in_dim(dec_len, micro_c, 0, keepdims=False)
            pre_begin = pre_len[0] + micro_c * seg_len
            pre_pos = pre_begin + jnp.arange(seg_len)
            positions = jnp.concatenate([dec_pos, pre_pos])
            hit = (cache_pos[None, :] == dec_pos[:, None])[:, :, None, None]
            dec_valid = (cache_pos[None, :] <= dec_pos[:, None])[:, None, None, :]
            pre_valid = (cache_pos[None, :] <= pre_pos[:, None])[:, None, None, :]
            for layer_idx in range(local_layers):
                normed = rms_norm(acts, g_attn[layer_idx])
                q_grp, k_new, v_new = project(normed, positions, w_q[layer_idx], w_k[layer_idx], w_v[layer_idx], kv_count, head_dim)
                kd_m = jnp.where(hit, k_new[:dec_rows, None], lax.dynamic_index_in_dim(kd_all[layer_idx], micro_c, 0, keepdims=False))
                vd_m = jnp.where(hit, v_new[:dec_rows, None], lax.dynamic_index_in_dim(vd_all[layer_idx], micro_c, 0, keepdims=False))
                kd_all = lax.dynamic_update_slice(kd_all, kd_m[None, None], (layer_idx, micro_c, 0, 0, 0, 0))
                vd_all = lax.dynamic_update_slice(vd_all, vd_m[None, None], (layer_idx, micro_c, 0, 0, 0, 0))
                kp_all = lax.dynamic_update_slice(kp_all, k_new[None, dec_rows:], (layer_idx, pre_begin, 0, 0))
                vp_all = lax.dynamic_update_slice(vp_all, v_new[None, dec_rows:], (layer_idx, pre_begin, 0, 0))
                attn_out = jnp.concatenate([
                    attend(q_grp[:dec_rows], kd_m, vd_m, dec_valid, 'bkgd,bskd->bkgs', 'bkgs,bskd->bkgd'),
                    attend(q_grp[dec_rows:], kp_all[layer_idx], vp_all[layer_idx], pre_valid, 'ikgd,skd->ikgs', 'ikgs,skd->ikgd')], axis=0)
                acts = finish(acts, attn_out, w_o[layer_idx], g_mlp[layer_idx], w_gate[layer_idx], w_up[layer_idx], w_down[layer_idx])
            return acts, (kd_all, vd_all, kp_all, vp_all)

        def keep_rows(acts):
            return jnp.concatenate([acts[:dec_rows], acts[-1:]], axis=0)

        src_rows = jnp.concatenate([x_dec, x_pre], axis=1)
        collect, caches = run_stages(src_rows, dec_rows + 1, keep_rows, stage_fn, (k_dec, v_dec, k_pre, v_pre), fwd_perm)
        last_rows = lax.psum(jnp.where(stage_idx == n_stages - 1, collect, jnp.zeros_like(collect)), 'stage')
        final_h = rms_norm(last_rows, g_final)
        logits = jnp.dot(final_h.reshape(-1, hidden), w_head, preferred_element_type=jnp.float32).reshape(n_micro, dec_rows + 1, -1)
        return (logits,) + caches

    return jax.shard_map(device_fn, mesh=mesh, in_specs=in_specs, out_specs=out_specs, check_vma=False)
```

profile of v0, /device:TPU:113, one launch (start us, length us, event | category | flops | bytes accessed | tf_op | source)
XLA Modules:
  0.0 759.8 jit_solution(4086313852875658655)
XLA Ops:
  7.2 8.4 %copy.113 = bf16[1,4,32,256,2,64]{3,5,4,2,1,0:T(8,128)(2,1)} copy(bf16[1,4,32,256,2,64]{3,5,4,2,1,0:T(8,128)(2,1)} %param.38) | data formatting | bytes 16777216
  15.7 8.5 %copy.114 = bf16[1,4,32,256,2,64]{3,5,4,2,1,0:T(8,128)(2,1)} copy(bf16[1,4,32,256,2,64]{3,5,4,2,1,0:T(8,128)(2,1)} %param.39) | data formatting | bytes 16777216
  24.9 2.9 copy.53
  30.8 496.8 %while.25 = (s32[]{:T(128)}, bf16[64,896]{1,0:T(8,128)(2,1)}, bf16[4,33,896]{2,1,0:T(8,128)(2,1)}, bf16[1,4,32,256,2,64]{3,5,4,2,1,0:T(8,128)(2,1)}, bf16[1,4,32...) while((s32[]{:T(128)}, bf16[64,896]{1,0:T(8,128)(2,1)}, ...), condition=%wide.region_9.10_spmd.clone.clone, body=%wide.region_0.9_spmd.clone.clone.sunk | while | flops 1992278784 | bytes 60374584 | solution.py:79
  30.8 4.6 collective-permute-start
  35.4 52.8 %collective-permute-done = bf16[64,896]{1,0:T(8,128)(2,1)S(1)} collective-permute-done((bf16[64,896]{1,0:T(8,128)(2,1)}, bf16[64,896]{1,0:T(8,128)(2,1)S(1)}, u32[]{:S(2)}, u32[]{:S(2)}) %collective-permute-start) | collective-permute-done | bytes 114720 | tf_op jit(solution)/shard_map/while/body/eval_jaxpr/ppermute | solution.py:76
  88.9 54.7 %conditional.4 = ((bf16[64,896]{1,0:T(8,128)(2,1)}, bf16[4,33,896]{2,1,0:T(8,128)(2,1)}, bf16[1,4,32,256,2,64]{3,5,4,2,1,0:T(8,128)(2,1)}, bf16[1,4,32,256,2,64]...) conditional(s32[]{:T(128)} %convert_element_type.150, ...), branch_computations={%region_1.1_spmd, %region_2.8_spmd} | conditional | flops 1992278784 | bytes 59684916 | solution.py:75
  99.9 1.8 dynamic_update_slice.15
  101.7 2.1 fusion.29
  103.8 2.8 fusion.46
  112.8 2.4 fusion.17
  116.8 3.0 fusion.33
  119.8 1.7 reshape.237
  122.8 4.8 fusion.8
  127.6 9.5 %fusion.37 = bf16[64,896]{1,0:T(8,128)(2,1)} fusion(f32[64,896]{1,0:T(8,128)S(1)} %get-tuple-element.734, bf16[1,4864,896]{2,1,0:T(8,128)(2,1)} %get-tuple-element.450, bf16[1,896,4864]{2,1,0:T(8,128)(2,1)} %get-tuple-element.449, f32[64,4864]{1,0:T(8,128)S(1)} %fusion.8, f32[896]{0:T(1024)} %get-tuple-element.736, f32[64]{0:T(128)S(1)} %add_rsqrt_fusion), kind=kOutput, calls=%fused_computation.33 | convolution fusion | flops 1117839360 | bytes 19025664 | tf_op jit(solution)/shard_map/while/body/eval_jaxpr/cond/branch_1_fun/dot_general | solution.py:53
  139.4 4.2 select_dynamic-update-slice_fusion
  143.6 1.9 collective-permute-start
  145.5 1.8 collective-permute-done
  147.9 54.4 %conditional.4 = ((bf16[64,896]{1,0:T(8,128)(2,1)}, bf16[4,33,896]{2,1,0:T(8,128)(2,1)}, bf16[1,4,32,256,2,64]{3,5,4,2,1,0:T(8,128)(2,1)}, bf16[1,4,32,256,2,64]...) conditional(s32[]{:T(128)} %convert_element_type.150, ...), branch_computations={%region_1.1_spmd, %region_2.8_spmd} | conditional | flops 1992278784 | bytes 59684916 | solution.py:75
  160.5 2.1 fusion.29
  162.6 2.8 fusion.46
  171.6 2.4 fusion.17
  175.6 3.0 fusion.33
  181.6 4.8 fusion.8
  186.4 9.5 %fusion.37 = bf16[64,896]{1,0:T(8,128)(2,1)} fusion(f32[64,896]{1,0:T(8,128)S(1)} %get-tuple-element.734, bf16[1,4864,896]{2,1,0:T(8,128)(2,1)} %get-tuple-element.450, bf16[1,896,4864]{2,1,0:T(8,128)(2,1)} %get-tuple-element.449, f32[64,4864]{1,0:T(8,128)S(1)} %fusion.8, f32[896]{0:T(1024)} %get-tuple-element.736, f32[64]{0:T(128)S(1)} %add_rsqrt_fusion), kind=kOutput, calls=%fused_computation.33 | convolution fusion | flops 1117839360 | bytes 19025664 | tf_op jit(solution)/shard_map/while/body/eval_jaxpr/cond/branch_1_fun/dot_general | solution.py:53
  198.2 4.2 select_dynamic-update-slice_fusion
  202.4 4.6 collective-permute-start
  207.0 1.8 collective-permute-done
  209.4 54.4 %conditional.4 = ((bf16[64,896]{1,0:T(8,128)(2,1)}, bf16[4,33,896]{2,1,0:T(8,128)(2,1)}, bf16[1,4,32,256,2,64]{3,5,4,2,1,0:T(8,128)(2,1)}, bf16[1,4,32,256,2,64]...) conditional(s32[]{:T(128)} %convert_element_type.150, ...), branch_computations={%region_1.1_spmd, %region_2.8_spmd} | conditional | flops 1992278784 | bytes 59684916 | solution.py:75
  221.9 2.1 fusion.29
  224.0 2.8 fusion.46
  233.1 2.4 fusion.17
  237.0 3.0 fusion.33
  243.0 4.8 fusion.8
  247.9 9.5 %fusion.37 = bf16[64,896]{1,0:T(8,128)(2,1)} fusion(f32[64,896]{1,0:T(8,128)S(1)} %get-tuple-element.734, bf16[1,4864,896]{2,1,0:T(8,128)(2,1)} %get-tuple-element.450, bf16[1,896,4864]{2,1,0:T(8,128)(2,1)} %get-tuple-element.449, f32[64,4864]{1,0:T(8,128)S(1)} %fusion.8, f32[896]{0:T(1024)} %get-tuple-element.736, f32[64]{0:T(128)S(1)} %add_rsqrt_fusion), kind=kOutput, calls=%fused_computation.33 | convolution fusion | flops 1117839360 | bytes 19025664 | tf_op jit(solution)/shard_map/while/body/eval_jaxpr/cond/branch_1_fun/dot_general | solution.py:53
  259.6 4.2 select_dynamic-update-slice_fusion
  263.8 4.4 collective-permute-start
  268.2 1.8 collective-permute-done
  270.6 54.4 %conditional.4 = ((bf16[64,896]{1,0:T(8,128)(2,1)}, bf16[4,33,896]{2,1,0:T(8,128)(2,1)}, bf16[1,4,32,256,2,64]{3,5,4,2,1,0:T(8,128)(2,1)}, bf16[1,4,32,256,2,64]...) conditional(s32[]{:T(128)} %convert_element_type.150, ...), branch_computations={%region_1.1_spmd, %region_2.8_spmd} | conditional | flops 1992278784 | bytes 59684916 | solution.py:75
  283.1 2.1 fusion.29
  285.2 2.8 fusion.46
  294.3 2.4 fusion.17
  298.2 3.0 fusion.33
  301.2 1.7 reshape.237
  304.2 4.8 fusion.8
  309.1 9.5 %fusion.37 = bf16[64,896]{1,0:T(8,128)(2,1)} fusion(f32[64,896]{1,0:T(8,128)S(1)} %get-tuple-element.734, bf16[1,4864,896]{2,1,0:T(8,128)(2,1)} %get-tuple-element.450, bf16[1,896,4864]{2,1,0:T(8,128)(2,1)} %get-tuple-element.449, f32[64,4864]{1,0:T(8,128)S(1)} %fusion.8, f32[896]{0:T(1024)} %get-tuple-element.736, f32[64]{0:T(128)S(1)} %add_rsqrt_fusion), kind=kOutput, calls=%fused_computation.33 | convolution fusion | flops 1117839360 | bytes 19025664 | tf_op jit(solution)/shard_map/while/body/eval_jaxpr/cond/branch_1_fun/dot_general | solution.py:53
  320.8 4.2 select_dynamic-update-slice_fusion
  325.0 4.4 collective-permute-start
  329.4 1.8 collective-permute-done
  331.8 58.8 %collective-permute-start = (bf16[64,896]{1,0:T(8,128)(2,1)}, bf16[64,896]{1,0:T(8,128)(2,1)S(1)}, u32[]{:S(2)}, u32[]{:S(2)}) collective-permute-start(bf16[64,896]{1,0:T(8,128)(2,1)} %get-tuple-element.865), channel_id=1, source_target_pairs={{0,1},{1,2},{2,3},{3,4},{4,5},{5,6},{6,7},{8,9},{9,10},{10,11},{11... | collective-permute-start | bytes 344072 | tf_op jit(solution)/shard_map/while/body/eval_jaxpr/ppermute | solution.py:76
  390.6 1.8 collective-permute-done
  393.0 4.3 collective-permute-start
  397.3 1.8 collective-permute-done
  399.8 52.7 %collective-permute-start = (bf16[64,896]{1,0:T(8,128)(2,1)}, bf16[64,896]{1,0:T(8,128)(2,1)S(1)}, u32[]{:S(2)}, u32[]{:S(2)}) collective-permute-start(bf16[64,896]{1,0:T(8,128)(2,1)} %get-tuple-element.865), channel_id=1, source_target_pairs={{0,1},{1,2},{2,3},{3,4},{4,5},{5,6},{6,7},{8,9},{9,10},{10,11},{11... | collective-permute-start | bytes 344072 | tf_op jit(solution)/shard_map/while/body/eval_jaxpr/ppermute | solution.py:76
  452.4 1.8 collective-permute-done
  454.8 4.3 collective-permute-start
  459.2 1.8 collective-permute-done
  461.6 56.9 %collective-permute-start = (bf16[64,896]{1,0:T(8,128)(2,1)}, bf16[64,896]{1,0:T(8,128)(2,1)S(1)}, u32[]{:S(2)}, u32[]{:S(2)}) collective-permute-start(bf16[64,896]{1,0:T(8,128)(2,1)} %get-tuple-element.865), channel_id=1, source_target_pairs={{0,1},{1,2},{2,3},{3,4},{4,5},{5,6},{6,7},{8,9},{9,10},{10,11},{11... | collective-permute-start | bytes 344072 | tf_op jit(solution)/shard_map/while/body/eval_jaxpr/ppermute | solution.py:76
  518.5 1.8 collective-permute-done
  520.9 4.3 collective-permute-start
  525.2 1.8 collective-permute-done
  529.1 210.8 %all-reduce.2.cloned.1.call-done = bf16[4,33,896]{2,1,0:T(8,128)(2,1)} async-done(((bf16[4,33,896]{2,1,0:T(8,128)(2,1)}), bf16[4,33,896]{2,1,0:T(8,128)(2,1)}) %all-reduce.2.cloned.1.call-update) | async-done | bytes 236560 | tf_op jit(solution)/shard_map/psum | solution.py:128
  741.0 7.1 fusion.95
  748.1 4.8 copy.55
  (257 shorter events, 107.6 us)
Async XLA Ops:
  7.2 732.8 %all-reduce.2.cloned.1.call-start = ((), (), s32[]{:S(2)}) async-start(), calls=%async_computation | async-start | bytes 573440 | tf_op jit(solution)/shard_map/psum | solution.py:128
  15.7 8.5 %copy-start.14 = (bf16[1,256,2,64]{1,3,2,0:T(8,128)(2,1)S(1)}, bf16[1,256,2,64]{1,3,2,0:T(8,128)(2,1)}, u32[]{:S(2)}) copy-start(bf16[1,256,2,64]{1,3,2,0:T(8,128)(2,1)} %param.41) | copy-start | bytes 196612
  15.7 12.1 %copy-start.13 = (bf16[1,896,128]{2,1,0:T(8,128)(2,1)S(1)}, bf16[1,896,128]{2,1,0:T(8,128)(2,1)}, u32[]{:S(2)}) copy-start(bf16[1,896,128]{2,1,0:T(8,128)(2,1)} %param.29) | copy-start | bytes 688132
  15.7 12.9 %copy-start.11 = (bf16[4,32,896]{2,1,0:T(8,128)(2,1)S(1)}, bf16[4,32,896]{2,1,0:T(8,128)(2,1)}, u32[]{:S(2)}) copy-start(bf16[4,32,896]{2,1,0:T(8,128)(2,1)} %param.24) | copy-start | bytes 688132
  15.7 12.9 %copy-start.12 = (bf16[4,32,896]{2,1,0:T(8,128)(2,1)S(1)}, bf16[4,32,896]{2,1,0:T(8,128)(2,1)}, u32[]{:S(2)}) copy-start(bf16[4,32,896]{2,1,0:T(8,128)(2,1)} %param.23) | copy-start | bytes 688132
  15.7 15.1 %copy-start.5 = (bf16[1,256,2,64]{1,3,2,0:T(8,128)(2,1)S(1)}, bf16[1,256,2,64]{1,3,2,0:T(8,128)(2,1)}, u32[]{:S(2)}) copy-start(bf16[1,256,2,64]{1,3,2,0:T(8,128)(2,1)} %param.40) | copy-start | bytes 196612
  30.8 57.4 %collective-permute-start = (bf16[64,896]{1,0:T(8,128)(2,1)}, bf16[64,896]{1,0:T(8,128)(2,1)S(1)}, u32[]{:S(2)}, u32[]{:S(2)}) collective-permute-start(bf16[64,896]{1,0:T(8,128)(2,1)} %get-tuple-element.865), channel_id=1, source_target_pairs={{0,1},{1,2},{2,3},{3,4},{4,5},{5,6},{6,7},{8,9},{9,10},{10,11},{11... | collective-permute-start | bytes 344072 | tf_op jit(solution)/shard_map/while/body/eval_jaxpr/ppermute | solution.py:76
  93.8 6.1 copy-start.1
  94.5 5.3 copy-start.10
  96.9 2.9 copy-start.2
  101.7 19.7 %copy-start = (bf16[1,896,896]{2,1,0:T(8,128)(2,1)S(1)}, bf16[1,896,896]{2,1,0:T(8,128)(2,1)}, u32[]{:S(2)}) copy-start(bf16[1,896,896]{2,1,0:T(8,128)(2,1)} %get-tuple-element.446) | copy-start | bytes 4816900 | tf_op jit(solution)/shard_map/while/body/eval_jaxpr/cond
  112.8 3.8 copy-start.6
  127.6 11.8 %copy-start.7 = (bf16[32,2,64]{2,1,0:T(2,128)(2,1)S(1)}, bf16[32,2,64]{2,1,0:T(2,128)(2,1)}, u32[]{:S(2)}) copy-start(bf16[32,2,64]{2,1,0:T(2,128)(2,1)} %copy-done.6) | copy-start | bytes 24580 | tf_op jit(solution)/shard_map/while/body/eval_jaxpr/cond
  127.6 11.8 %copy-start.8 = (bf16[32,2,64]{2,1,0:T(2,128)(2,1)S(1)}, bf16[32,2,64]{2,1,0:T(2,128)(2,1)}, u32[]{:S(2)}) copy-start(bf16[32,2,64]{2,1,0:T(2,128)(2,1)} %broadcast_in_dim.92) | copy-start | bytes 24580 | tf_op jit(solution)/shard_map/while/body/eval_jaxpr/cond
  127.6 11.8 %copy-start.9 = (pred[32,256]{1,0:T(8,128)(4,1)S(1)}, pred[32,256]{1,0:T(8,128)(4,1)}, u32[]{:S(2)}) copy-start(pred[32,256]{1,0:T(8,128)(4,1)} %get-tuple-element.730) | copy-start | bytes 24580 | tf_op jit(solution)/shard_map/while/body/eval_jaxpr/cond
  137.2 6.4 copy-start.3
  143.6 3.7 collective-permute-start
  152.8 6.0 copy-start.1
  153.5 5.3 copy-start.10
  155.9 2.9 copy-start.2
  160.5 19.7 %copy-start = (bf16[1,896,896]{2,1,0:T(8,128)(2,1)S(1)}, bf16[1,896,896]{2,1,0:T(8,128)(2,1)}, u32[]{:S(2)}) copy-start(bf16[1,896,896]{2,1,0:T(8,128)(2,1)} %get-tuple-element.446) | copy-start | bytes 4816900 | tf_op jit(solution)/shard_map/while/body/eval_jaxpr/cond
  171.6 3.8 copy-start.6
  186.4 11.8 %copy-start.7 = (bf16[32,2,64]{2,1,0:T(2,128)(2,1)S(1)}, bf16[32,2,64]{2,1,0:T(2,128)(2,1)}, u32[]{:S(2)}) copy-start(bf16[32,2,64]{2,1,0:T(2,128)(2,1)} %copy-done.6) | copy-start | bytes 24580 | tf_op jit(solution)/shard_map/while/body/eval_jaxpr/cond
  186.4 11.8 %copy-start.8 = (bf16[32,2,64]{2,1,0:T(2,128)(2,1)S(1)}, bf16[32,2,64]{2,1,0:T(2,128)(2,1)}, u32[]{:S(2)}) copy-start(bf16[32,2,64]{2,1,0:T(2,128)(2,1)} %broadcast_in_dim.92) | copy-start | bytes 24580 | tf_op jit(solution)/shard_map/while/body/eval_jaxpr/cond
  186.4 11.8 %copy-start.9 = (pred[32,256]{1,0:T(8,128)(4,1)S(1)}, pred[32,256]{1,0:T(8,128)(4,1)}, u32[]{:S(2)}) copy-start(pred[32,256]{1,0:T(8,128)(4,1)} %get-tuple-element.730) | copy-start | bytes 24580 | tf_op jit(solution)/shard_map/while/body/eval_jaxpr/cond
  196.0 6.4 copy-start.3
  202.4 6.4 collective-permute-start
  214.3 6.0 copy-start.1
  215.0 5.3 copy-start.10
  217.4 2.9 copy-start.2
  221.9 19.7 %copy-start = (bf16[1,896,896]{2,1,0:T(8,128)(2,1)S(1)}, bf16[1,896,896]{2,1,0:T(8,128)(2,1)}, u32[]{:S(2)}) copy-start(bf16[1,896,896]{2,1,0:T(8,128)(2,1)} %get-tuple-element.446) | copy-start | bytes 4816900 | tf_op jit(solution)/shard_map/while/body/eval_jaxpr/cond
  233.1 3.8 copy-start.6
  247.8 11.8 %copy-start.7 = (bf16[32,2,64]{2,1,0:T(2,128)(2,1)S(1)}, bf16[32,2,64]{2,1,0:T(2,128)(2,1)}, u32[]{:S(2)}) copy-start(bf16[32,2,64]{2,1,0:T(2,128)(2,1)} %copy-done.6) | copy-start | bytes 24580 | tf_op jit(solution)/shard_map/while/body/eval_jaxpr/cond
  247.8 11.8 %copy-start.8 = (bf16[32,2,64]{2,1,0:T(2,128)(2,1)S(1)}, bf16[32,2,64]{2,1,0:T(2,128)(2,1)}, u32[]{:S(2)}) copy-start(bf16[32,2,64]{2,1,0:T(2,128)(2,1)} %broadcast_in_dim.92) | copy-start | bytes 24580 | tf_op jit(solution)/shard_map/while/body/eval_jaxpr/cond
  247.9 11.8 %copy-start.9 = (pred[32,256]{1,0:T(8,128)(4,1)S(1)}, pred[32,256]{1,0:T(8,128)(4,1)}, u32[]{:S(2)}) copy-start(pred[32,256]{1,0:T(8,128)(4,1)} %get-tuple-element.730) | copy-start | bytes 24580 | tf_op jit(solution)/shard_map/while/body/eval_jaxpr/cond
  257.4 6.4 copy-start.3
  263.8 6.1 collective-permute-start
  275.5 6.0 copy-start.1
  276.2 5.3 copy-start.10
  278.6 2.9 copy-start.2
  283.1 19.7 %copy-start = (bf16[1,896,896]{2,1,0:T(8,128)(2,1)S(1)}, bf16[1,896,896]{2,1,0:T(8,128)(2,1)}, u32[]{:S(2)}) copy-start(bf16[1,896,896]{2,1,0:T(8,128)(2,1)} %get-tuple-element.446) | copy-start | bytes 4816900 | tf_op jit(solution)/shard_map/while/body/eval_jaxpr/cond
  294.3 3.8 copy-start.6
  309.0 11.8 %copy-start.7 = (bf16[32,2,64]{2,1,0:T(2,128)(2,1)S(1)}, bf16[32,2,64]{2,1,0:T(2,128)(2,1)}, u32[]{:S(2)}) copy-start(bf16[32,2,64]{2,1,0:T(2,128)(2,1)} %copy-done.6) | copy-start | bytes 24580 | tf_op jit(solution)/shard_map/while/body/eval_jaxpr/cond
  309.0 11.8 %copy-start.8 = (bf16[32,2,64]{2,1,0:T(2,128)(2,1)S(1)}, bf16[32,2,64]{2,1,0:T(2,128)(2,1)}, u32[]{:S(2)}) copy-start(bf16[32,2,64]{2,1,0:T(2,128)(2,1)} %broadcast_in_dim.92) | copy-start | bytes 24580 | tf_op jit(solution)/shard_map/while/body/eval_jaxpr/cond
  309.1 11.8 %copy-start.9 = (pred[32,256]{1,0:T(8,128)(4,1)S(1)}, pred[32,256]{1,0:T(8,128)(4,1)}, u32[]{:S(2)}) copy-start(pred[32,256]{1,0:T(8,128)(4,1)} %get-tuple-element.730) | copy-start | bytes 24580 | tf_op jit(solution)/shard_map/while/body/eval_jaxpr/cond
  318.6 6.4 copy-start.3
  325.0 6.1 collective-permute-start
  331.8 60.6 %collective-permute-start = (bf16[64,896]{1,0:T(8,128)(2,1)}, bf16[64,896]{1,0:T(8,128)(2,1)S(1)}, u32[]{:S(2)}, u32[]{:S(2)}) collective-permute-start(bf16[64,896]{1,0:T(8,128)(2,1)} %get-tuple-element.865), channel_id=1, source_target_pairs={{0,1},{1,2},{2,3},{3,4},{4,5},{5,6},{6,7},{8,9},{9,10},{10,11},{11... | collective-permute-start | bytes 344072 | tf_op jit(solution)/shard_map/while/body/eval_jaxpr/ppermute | solution.py:76
  393.0 6.1 collective-permute-start
  399.8 54.4 %collective-permute-start = (bf16[64,896]{1,0:T(8,128)(2,1)}, bf16[64,896]{1,0:T(8,128)(2,1)S(1)}, u32[]{:S(2)}, u32[]{:S(2)}) collective-permute-start(bf16[64,896]{1,0:T(8,128)(2,1)} %get-tuple-element.865), channel_id=1, source_target_pairs={{0,1},{1,2},{2,3},{3,4},{4,5},{5,6},{6,7},{8,9},{9,10},{10,11},{11... | collective-permute-start | bytes 344072 | tf_op jit(solution)/shard_map/while/body/eval_jaxpr/ppermute | solution.py:76
  454.8 6.1 collective-permute-start
  461.6 58.6 %collective-permute-start = (bf16[64,896]{1,0:T(8,128)(2,1)}, bf16[64,896]{1,0:T(8,128)(2,1)S(1)}, u32[]{:S(2)}, u32[]{:S(2)}) collective-permute-start(bf16[64,896]{1,0:T(8,128)(2,1)} %get-tuple-element.865), channel_id=1, source_target_pairs={{0,1},{1,2},{2,3},{3,4},{4,5},{5,6},{6,7},{8,9},{9,10},{10,11},{11... | collective-permute-start | bytes 344072 | tf_op jit(solution)/shard_map/while/body/eval_jaxpr/ppermute | solution.py:76
  520.9 6.1 collective-permute-start
  527.6 220.5 %copy-start.4 = (bf16[1,256,2,64]{1,3,2,0:T(8,128)(2,1)}, bf16[1,256,2,64]{1,3,2,0:T(8,128)(2,1)S(1)}, u32[]{:S(2)}) copy-start(bf16[1,256,2,64]{1,3,2,0:T(8,128)(2,1)S(1)} %get-tuple-element.671) | copy-start | bytes 196612
Sparse Core Ops, SparseCore 0:
  528.6 211.3 all-reduce.1
where the time goes:
time: 764 us; the launch traced here: 760 us
  waiting for transfers between devices  281 us (37%)
  starting transfers between devices  201 us (26%)
  matrix products  127 us (17%)
  local copies, waits for them, and re-layouts  86.9 us (11%)
  other arithmetic  45.5 us (6%)
  between operations  14.1 us (2%)
    psum x1, waiting for transfers between devices, device_fn(): lax.psum(jnp.where(stage_idx == n_stages - 1, collect, jnp.zeros_like(col...  211 us
    ppermute x11, starting transfers between devices, tick_fn(): return (lax.ppermute(sent_rows, 'stage', fwd_perm), collect, cache_state)  201 us
    ppermute x11, waiting for transfers between devices, tick_fn(): return (lax.ppermute(sent_rows, 'stage', fwd_perm), collect, cache_state)  70.6 us
    dot_general x4, matrix products, finish(): jnp.dot(hidden_act, wd_l, preferred_element_type=jnp.float32)  38.2 us
    unnamed x18, local copies, waits for them, and re-layouts  26.2 us
    dot_general x8, matrix products, attend(): jnp.einsum(mix_form, probs, values_in, preferred_element_type=jnp.float32)  22.9 us
    dot_general x4, matrix products, finish(): gate_f = jnp.dot(normed, wg_l, preferred_element_type=jnp.float32)  19.4 us
    dot_general x8, matrix products, attend(): jnp.einsum(score_form, q_grp, keys_in, preferred_element_type=jnp.float32)  18.1 us
  transfers between devices with their start and end apart: 12, of which 12 were waited for; matrix products, arithmetic and copies ran while one was open for 0% of the time, Pallas kernels for 0%

commit v1 on v0

v1 whole, which is shorter than its diff:
```python
import functools

import jax
import jax.numpy as jnp
import numpy as np
from jax import lax
from jax.experimental import pallas as pl
from jax.experimental.pallas import tpu as pltpu
from jax.sharding import PartitionSpec as P

NORM_EPS = 1e-6
ROPE_BASE = 10000.0
F32 = jnp.float32
BF16 = jnp.bfloat16
NEG = -1e30
HBM = pl.ANY
VMEM = pltpu.VMEM
SMEM = pltpu.SMEM
MESH = pl.DeviceIdType.MESH


def rms_norm(acts, gain):
    acts_f = acts.astype(F32)
    inv_rms = lax.rsqrt(jnp.mean(acts_f * acts_f, axis=-1, keepdims=True) + NORM_EPS)
    return (acts_f * inv_rms * gain.astype(F32)).astype(BF16)


def dot(lhs, rhs):
    return jnp.dot(lhs, rhs, preferred_element_type=F32)


def dot_t(lhs, rhs):
    return lax.dot_general(lhs, rhs, (((1,), (1,)), ((), ())), preferred_element_type=F32)


def softmax(scores):
    expd = jnp.exp(scores - jnp.max(scores, axis=-1, keepdims=True))
    return expd * (1.0 / jnp.sum(expd, axis=-1, keepdims=True))


def pipeline_kernel(
    n_stages,
    dec_len, pre_len, inv_freq, g_attn, g_mlp, g_final,
    x_dec, x_pre, w_q, w_k, w_v, w_o, w_gate, w_up, w_down, k_dec, v_dec, k_pre, v_pre,
    fin_out, kn_out, vn_out, kp_out, vp_out,
    wqkv, wo, w1, w3, w2, kc, vc, kp, vp, xin, xout, fin, qd, od, kn, vn, cosv, sinv, hid,
    w_sem, kv_sem, p_sem, x_sem, o_sem, send_sem, recv_sem, fsend_sem, frecv_sem,
):
    n_micro, n_rows, hidden = xin.shape
    dec_rows = x_dec.shape[1]
    seg_len = x_pre.shape[1]
    kv_width, cache_len = kp.shape
    q_width = wo.shape[0]
    ffn = w1.shape[1]
    head_dim = 64
    kv_count = kv_width // head_dim
    q_heads = q_width // head_dim
    group = q_heads // kv_count
    stage = lax.axis_index('stage')
    last = n_stages - 1
    half = ffn // 2

    barrier = pltpu.get_barrier_semaphore()

    def x_copies(m):
        return (
            pltpu.make_async_copy(x_dec.at[m], xin.at[m, pl.ds(0, dec_rows)], x_sem.at[m, 0]),
            pltpu.make_async_copy(x_pre.at[m], xin.at[m, pl.ds(dec_rows, seg_len)], x_sem.at[m, 1]),
        )

    def kv_copies(m):
        return (
            pltpu.make_async_copy(k_dec.at[m], kc.at[m], kv_sem.at[m, 0]),
            pltpu.make_async_copy(v_dec.at[m], vc.at[m], kv_sem.at[m, 1]),
        )

    qkv_copies = (
        pltpu.make_async_copy(w_q, wqkv.at[:, pl.ds(0, q_width)], w_sem.at[0]),
        pltpu.make_async_copy(w_k, wqkv.at[:, pl.ds(q_width, kv_width)], w_sem.at[1]),
        pltpu.make_async_copy(w_v, wqkv.at[:, pl.ds(q_width + kv_width, kv_width)], w_sem.at[2]),
    )
    pre_copies = (
        pltpu.make_async_copy(k_pre, kp, p_sem.at[0]),
        pltpu.make_async_copy(v_pre, vp, p_sem.at[1]),
    )
    wo_copies = (pltpu.make_async_copy(w_o, wo, w_sem.at[3]),)
    up_copies = tuple(
        (
            pltpu.make_async_copy(w_gate.at[:, pl.ds(i * half, half)], w1.at[:, pl.ds(i * half, half)], w_sem.at[4 + 2 * i]),
            pltpu.make_async_copy(w_up.at[:, pl.ds(i * half, half)], w3.at[:, pl.ds(i * half, half)], w_sem.at[5 + 2 * i]),
        )
        for i in range(2)
    )
    down_copies = (pltpu.make_async_copy(w_down, w2, w_sem.at[8]),)

    @pl.when(stage == 0)
    def _():
        for copy in x_copies(0):
            copy.start()
    for copy in qkv_copies + pre_copies + kv_copies(0) + wo_copies + up_copies[0] + up_copies[1] + down_copies:
        copy.start()

    @pl.when(stage == 0)
    def _():
        for m in range(1, n_micro):
            for copy in x_copies(m):
                copy.start()
    for m in range(1, n_micro):
        for copy in kv_copies(m):
            copy.start()

    @pl.when(stage > 0)
    def _():
        pl.semaphore_signal(barrier, inc=1, device_id={'stage': stage - 1}, device_id_type=MESH)

    @pl.when(stage < last)
    def _():
        pl.semaphore_signal(barrier, inc=1, device_id={'stage': last}, device_id_type=MESH)

    lane = lax.broadcasted_iota(jnp.int32, (8, 128), 1)
    row8 = lax.broadcasted_iota(jnp.int32, (8, 128), 0)
    freq = inv_freq[...]
    sign = jnp.where((lane % head_dim) < head_dim // 2, -1.0, 1.0)

    def table_body(m, carry):
        for g in range(n_rows // 8):
            if g < dec_rows // 8:
                pos = jnp.zeros((8, 128), jnp.int32)
                for r in range(8):
                    pos = jnp.where(row8 == r, dec_len[m, g * 8 + r], pos)
            else:
                pos = pre_len[0] + m * seg_len + (g * 8 - dec_rows) + row8
            angle = pos.astype(F32) * freq
            cosv[m, pl.ds(g * 8, 8), :] = jnp.cos(angle)
            sinv[m, pl.ds(g * 8, 8), :] = jnp.sin(angle) * sign
        return carry

    lax.fori_loop(0, n_micro, table_body, 0)
    qd[...] = jnp.zeros(qd.shape, F32)

    @pl.when(stage < last)
    def _():
        pl.semaphore_wait(barrier, 1)

    @pl.when(stage == last)
    def _():
        pl.semaphore_wait(barrier, n_stages - 1)

    def x_send(m):
        return pltpu.make_async_remote_copy(
            src_ref=xout.at[m], dst_ref=xin.at[m], send_sem=send_sem.at[m], recv_sem=recv_sem.at[m],
            device_id={'stage': jnp.minimum(stage + 1, last)}, device_id_type=MESH)

    def fin_send(m, target):
        return pltpu.make_async_remote_copy(
            src_ref=fin.at[m], dst_ref=fin.at[m], send_sem=fsend_sem.at[m, target], recv_sem=frecv_sem.at[m],
            device_id={'stage': target}, device_id_type=MESH)

    def tick(m, carry):
        first = m == 0

        @pl.when(stage == 0)
        def _():
            for copy in x_copies(m):
                copy.wait()

        @pl.when(stage > 0)
        def _():
            x_send(m).wait_recv()

        @pl.when(first)
        def _():
            for copy in qkv_copies + pre_copies:
                copy.wait()

        acts = xin[m]
        normed = rms_norm(acts, g_attn[...])
        cosine = cosv[m]
        sine = sinv[m]
        lane_q = lax.broadcasted_iota(jnp.int32, (n_rows, 128), 1)
        low32 = (lane_q % head_dim) < head_dim // 2
        low_half = lax.broadcasted_iota(jnp.int32, (dec_rows, 128), 1) < head_dim

        def rotate(tile):
            swapped = jnp.where(low32, pltpu.roll(tile, 128 - head_dim // 2, 1), pltpu.roll(tile, head_dim // 2, 1))
            return tile * cosine + swapped * sine

        proj = dot(normed, wqkv[...])
        q_tiles = [rotate(proj[:, t * 128:(t + 1) * 128]).astype(BF16).astype(F32) for t in range(q_width // 128)]
        k_new = rotate(proj[:, q_width:q_width + kv_width]).astype(BF16)
        v_new = proj[:, q_width + kv_width:].astype(BF16)
        kn[...] = k_new[:dec_rows].astype(F32)
        vn[...] = v_new[:dec_rows].astype(F32)
        kn_out[m] = k_new[:dec_rows]
        vn_out[m] = v_new[:dec_rows]

        for j in range(q_heads):
            tile = q_tiles[j // 2][:dec_rows]
            if j % 2 != j // group:
                tile = pltpu.roll(tile, head_dim, 1)
            keep = low_half if j // group == 0 else jnp.logical_not(low_half)
            qd[pl.ds(j, dec_rows, stride=16), :] = jnp.where(keep, tile, 0.0)

        pre_begin = pre_len[0] + m * seg_len
        seg_row = lax.broadcasted_iota(jnp.int32, (seg_len, cache_len), 0)
        seg_col = lax.broadcasted_iota(jnp.int32, (seg_len, cache_len), 1)
        spread = (seg_col == seg_row + pre_begin).astype(F32).astype(BF16)
        col = lax.broadcasted_iota(jnp.int32, (kv_width, cache_len), 1)
        written = (col >= pre_begin) & (col < pre_begin + seg_len)
        contract0 = (((0,), (0,)), ((), ()))
        k_put = lax.dot_general(k_new[dec_rows:], spread, contract0, preferred_element_type=F32)
        v_put = lax.dot_general(v_new[dec_rows:], spread, contract0, preferred_element_type=F32)
        kp_f = jnp.where(written, k_put, kp[...].astype(F32)).astype(BF16)
        vp_f = jnp.where(written, v_put, vp[...].astype(F32)).astype(BF16)
        kp[...] = kp_f
        vp[...] = vp_f

        scale = head_dim ** -0.5
        pre_valid = seg_col <= seg_row + pre_begin
        valid_g = jnp.concatenate([pre_valid] * group, axis=0)
        pre_heads = []
        for g in range(kv_count):
            rows = []
            for j in range(g * group, (g + 1) * group):
                keep = low_half if j % 2 == 0 else jnp.logical_not(low_half)
                rows.append(jnp.where(keep, q_tiles[j // 2][dec_rows:], 0.0).astype(BF16))
            q_g = jnp.concatenate(rows, axis=0)
            k_g = kp_f[g * head_dim:(g + 1) * head_dim]
            v_g = vp_f[g * head_dim:(g + 1) * head_dim]
            scores = dot(q_g, jnp.concatenate([k_g, k_g], axis=0)) * scale
            probs = softmax(jnp.where(valid_g, scores, NEG)).astype(BF16)
            mixed = dot_t(probs, jnp.concatenate([v_g, v_g], axis=0))
            pre_heads += [mixed[i * seg_len:(i + 1) * seg_len] for i in range(group)]

        for copy in kv_copies(m):
            copy.wait()
        pos_lane = lax.broadcasted_iota(jnp.int32, (16, cache_len), 1)
        for b in range(dec_rows):
            pos = dec_len[m, b]
            q_b = qd[b * 16:(b + 1) * 16, :]
            s_old = dot(q_b.astype(BF16), kc[m, b]) * scale
            s_new = jnp.sum(q_b * kn[b:b + 1, :], axis=-1, keepdims=True) * scale
            here = pos_lane == pos
            scores = jnp.where(here, s_new, jnp.where(pos_lane < pos, s_old, NEG))
            peak = jnp.max(scores, axis=-1, keepdims=True)
            expd = jnp.exp(scores - peak)
            inv = 1.0 / jnp.sum(expd, axis=-1, keepdims=True)
            p_old = jnp.where(here, 0.0, expd * inv).astype(BF16)
            p_new = (jnp.exp(s_new - peak) * inv).astype(BF16).astype(F32)
            od[b * 16:(b + 1) * 16, :] = dot_t(p_old, vc[m, b]) + p_new * vn[b:b + 1, :]

        att_tiles = []
        for t in range(q_width // 128):
            parts = []
            for j in (2 * t, 2 * t + 1):
                part = od[pl.ds(j, dec_rows, stride=16), :]
                if j % 2 != j // group:
                    part = pltpu.roll(part, head_dim, 1)
                parts.append(part)
            dec_tile = jnp.where(low_half, parts[0], parts[1])
            pre_tile = jnp.where(low_half, pre_heads[2 * t], pre_heads[2 * t + 1])
            att_tiles.append(jnp.concatenate([dec_tile, pre_tile], axis=0).astype(BF16))
        att = jnp.concatenate(att_tiles, axis=1)

        @pl.when(first)
        def _():
            for copy in wo_copies:
                copy.wait()

        acts = (acts.astype(F32) + dot(att, wo[...])).astype(BF16)
        normed = rms_norm(acts, g_mlp[...])

        n_blk = 256
        for i in range(2):
            @pl.when(first)
            def _():
                for copy in up_copies[i]:
                    copy.wait()
            lo = 0 if i == 0 else half // n_blk * n_blk
            hi = half // n_blk * n_blk if i == 0 else ffn
            for n in range(lo, hi, n_blk):
                gate = dot(normed, w1[:, n:n + n_blk])
                up = dot(normed, w3[:, n:n + n_blk])
                hid[:, n:n + n_blk] = (jax.nn.silu(gate) * up).astype(BF16)

        @pl.when(first)
        def _():
            for copy in down_copies:
                copy.wait()
        acts = (acts.astype(F32) + dot(hid[...], w2[...])).astype(BF16)

        @pl.when(stage < last)
        def _():
            xout[m] = acts
            x_send(m).start()

        @pl.when(stage == last)
        def _():
            tail = jnp.concatenate([acts[:dec_rows], acts[n_rows - 8:]], axis=0)
            fin[m] = rms_norm(tail, g_final[...])
            for target in range(n_stages - 1):
                fin_send(m, target).start()
        return carry

    lax.fori_loop(0, n_micro, tick, 0)

    kp_copy = pltpu.make_async_copy(kp, kp_out, o_sem.at[0])
    vp_copy = pltpu.make_async_copy(vp, vp_out, o_sem.at[1])
    kp_copy.start()
    vp_copy.start()

    @pl.when(stage < last)
    def _():
        for m in range(n_micro):
            x_send(m).wait_send()
        for m in range(n_micro):
            fin_send(m, 0).wait_recv()

    @pl.when(stage == last)
    def _():
        for m in range(n_micro):
            for target in range(n_stages - 1):
                fin_send(m, target).wait_send()

    fin_copy = pltpu.make_async_copy(fin, fin_out, o_sem.at[2])
    fin_copy.start()
    kp_copy.wait()
    vp_copy.wait()
    fin_copy.wait()


def head_kernel(fin, w_head, logits, rows):
    n_micro = fin.shape[0]
    n_kept = logits.shape[0]

    @pl.when(pl.program_id(0) == 0)
    def _():
        for m in range(n_micro):
            kept = fin[m].astype(F32)
            for t in range(rows.shape[0]):
                tile = kept[:, t * 128:(t + 1) * 128]
                rows[t, pl.ds(m, n_kept - 1, stride=n_micro), :] = tile[:n_kept - 1]
                rows[t, (n_kept - 1) * n_micro + m:(n_kept - 1) * n_micro + m + 1, :] = tile[fin.shape[1] - 1:]

    lhs = jnp.concatenate([rows[t].astype(BF16) for t in range(rows.shape[0])], axis=1)
    out = dot(lhs, w_head[...])
    for i in range(n_kept):
        logits[i] = out[i * n_micro:(i + 1) * n_micro]


def cache_kernel(dec_len, kn, vn, k_in, v_in, k_out, v_out):
    n_seq, kv_width, cache_len = k_in.shape[1:]
    m = pl.program_id(0)
    first = pl.program_id(1) * n_seq
    col = lax.broadcasted_iota(jnp.int32, (kv_width, cache_len), 1)
    for new, old, out in ((kn, k_in, k_out), (vn, v_in, v_out)):
        cols = jnp.transpose(new[0].astype(F32))
        for b in range(n_seq):
            here = col == dec_len[m, first + b]
            out[0, b] = jnp.where(here, cols[:, b:b + 1], old[0, b].astype(F32)).astype(BF16)


def solution(mesh):
    n_stages = mesh.shape['stage']
    part_spec = P('replica')
    layer_spec = P('stage')
    cache_spec = P('stage', 'replica')
    in_specs = (part_spec,) * 4 + (layer_spec,) * 9 + (P(), P()) + (cache_spec,) * 4
    out_specs = (part_spec,) + (cache_spec,) * 4

    def device_fn(x_dec, x_pre, dec_len, pre_len, g_attn, w_q, w_k, w_v, w_o, g_mlp, w_gate, w_up, w_down, g_final, w_head, k_dec, v_dec, k_pre, v_pre):
        n_micro, dec_rows, hidden = x_dec.shape
        seg_len = x_pre.shape[1]
        n_rows = dec_rows + seg_len
        _, cache_len, kv_count, head_dim = k_pre.shape
        kv_width = kv_count * head_dim
        q_width = w_q.shape[2]
        ffn = w_gate.shape[2]
        vocab = w_head.shape[1]
        fin_rows = dec_rows + 8

        kd = jnp.transpose(k_dec[0], (0, 1, 3, 4, 2)).reshape(n_micro, dec_rows, kv_width, cache_len)
        vd = jnp.transpose(v_dec[0], (0, 1, 3, 4, 2)).reshape(n_micro, dec_rows, kv_width, cache_len)
        kpre = jnp.transpose(k_pre[0], (1, 2, 0)).reshape(kv_width, cache_len)
        vpre = jnp.transpose(v_pre[0], (1, 2, 0)).reshape(kv_width, cache_len)

        lanes = np.arange(128) % (head_dim // 2)
        inv_freq = jnp.asarray((ROPE_BASE ** (-lanes * (2.0 / head_dim))).astype(np.float32)[None, :])

        def spec(space):
            return pl.BlockSpec(memory_space=space)

        fin, kn, vn, kp, vp = pl.pallas_call(
            functools.partial(pipeline_kernel, n_stages),
            out_shape=(
                jax.ShapeDtypeStruct((n_micro, fin_rows, hidden), BF16),
                jax.ShapeDtypeStruct((n_micro, dec_rows, kv_width), BF16),
                jax.ShapeDtypeStruct((n_micro, dec_rows, kv_width), BF16),
                jax.ShapeDtypeStruct((kv_width, cache_len), BF16),
                jax.ShapeDtypeStruct((kv_width, cache_len), BF16),
            ),
            in_specs=[spec(SMEM)] * 2 + [spec(VMEM)] * 4 + [spec(HBM)] * 13,
            out_specs=(spec(HBM), spec(VMEM), spec(VMEM), spec(HBM), spec(HBM)),
            scratch_shapes=[
                VMEM((hidden, q_width + 2 * kv_width), BF16),
                VMEM((q_width, hidden), BF16),
                VMEM((hidden, ffn), BF16),
                VMEM((hidden, ffn), BF16),
                VMEM((ffn, hidden), BF16),
                VMEM((n_micro, dec_rows, kv_width, cache_len), BF16),
                VMEM((n_micro, dec_rows, kv_width, cache_len), BF16),
                VMEM((kv_width, cache_len), BF16),
                VMEM((kv_width, cache_len), BF16),
                VMEM((n_micro, n_rows, hidden), BF16),
                VMEM((n_micro, n_rows, hidden), BF16),
                VMEM((n_micro, fin_rows, hidden), BF16),
                VMEM((dec_rows * 16, 128), F32),
                VMEM((dec_rows * 16, 128), F32),
                VMEM((dec_rows, kv_width), F32),
                VMEM((dec_rows, kv_width), F32),
                VMEM((n_micro, n_rows, 128), F32),
                VMEM((n_micro, n_rows, 128), F32),
                VMEM((n_rows, ffn), BF16),
                pltpu.SemaphoreType.DMA((9,)),
                pltpu.SemaphoreType.DMA((n_micro, 2)),
                pltpu.SemaphoreType.DMA((2,)),
                pltpu.SemaphoreType.DMA((n_micro, 2)),
                pltpu.SemaphoreType.DMA((3,)),
                pltpu.SemaphoreType.DMA((n_micro,)),
                pltpu.SemaphoreType.DMA((n_micro,)),
                pltpu.SemaphoreType.DMA((n_micro, n_stages - 1)),
                pltpu.SemaphoreType.DMA((n_micro,)),
            ],
            compiler_params=pltpu.CompilerParams(collective_id=0, has_side_effects=True, vmem_limit_bytes=62 * 1024 * 1024),
            name='pipeline',
        )(dec_len, pre_len, inv_freq, g_attn, g_mlp, g_final.reshape(1, hidden),
          x_dec, x_pre, w_q[0], w_k[0], w_v[0], w_o[0], w_gate[0], w_up[0], w_down[0], kd, vd, kpre, vpre)

        v_blk = 1024
        logits = pl.pallas_call(
            head_kernel,
            grid=(vocab // v_blk,),
            out_shape=jax.ShapeDtypeStruct((dec_rows + 1, n_micro, vocab), F32),
            in_specs=[
                pl.BlockSpec((n_micro, fin_rows, hidden), lambda n: (0, 0, 0)),
                pl.BlockSpec((hidden, v_blk), lambda n: (0, n)),
            ],
            out_specs=pl.BlockSpec((dec_rows + 1, n_micro, v_blk), lambda n: (0, 0, n)),
            scratch_shapes=[VMEM((hidden // 128, (dec_rows + 1) * n_micro, 128), F32)],
            name='head',
        )(fin, w_head)

        n_seq = 8
        new_spec = pl.BlockSpec((1, n_seq, kv_width), lambda m, b: (m, b, 0))
        cache_blk = pl.BlockSpec((1, n_seq, kv_width, cache_len), lambda m, b: (m, b, 0, 0))
        kd_out, vd_out = pl.pallas_call(
            cache_kernel,
            grid=(n_micro, dec_rows // n_seq),
            out_shape=(jax.ShapeDtypeStruct(kd.shape, BF16),) * 2,
            in_specs=[spec(SMEM), new_spec, new_spec, cache_blk, cache_blk],
            out_specs=(cache_blk, cache_blk),
            name='cache',
        )(dec_len, kn, vn, kd, vd)

        def dec_cache(arr):
            return jnp.transpose(arr.reshape(n_micro, dec_rows, kv_count, head_dim, cache_len), (0, 1, 4, 2, 3))[None]

        def pre_cache(arr):
            return jnp.transpose(arr.reshape(kv_count, head_dim, cache_len), (2, 0, 1))[None]

        return jnp.transpose(logits, (1, 0, 2)), dec_cache(kd_out), dec_cache(vd_out), pre_cache(kp), pre_cache(vp)

    return jax.shard_map(device_fn, mesh=mesh, in_specs=in_specs, out_specs=out_specs, check_vma=False)
```

time: 764 us -> 204 us (0.27)
  waiting for transfers between devices: 281 us -> 0 us
  starting transfers between devices: 201 us -> 0 us
  Pallas kernels: 0 us -> 199 us
  matrix products: 127 us -> 0 us
  local copies, waits for them, and re-layouts: 86.9 us -> 2.53 us
  other arithmetic: 45.5 us -> 0 us
  between operations: 14.1 us -> 1.29 us
    psum x1 -> x0, waiting for transfers between devices: 211 us -> none  [device_fn(): lax.psum(jnp.where(stage_idx == n_stages - 1, collect, jnp.zeros_like(col...]
    ppermute x11 -> x0, starting transfers between devices: 201 us -> none  [tick_fn(): return (lax.ppermute(sent_rows, 'stage', fwd_perm), collect, cache_state)]
    pallas_call x0 -> x3, Pallas kernels: none -> 199 us  [the longest x1 169 us: device_fn(): pl.pallas_call(functools.partial(pipeline_kernel, n_stages), out_shape=(j...]
    dot_general x41 -> x0, matrix products: 123 us -> none  [the longest x4 38.2 us: finish(): jnp.dot(hidden_act, wd_l, preferred_element_type=jnp.float32)]
    ppermute x11 -> x0, waiting for transfers between devices: 70.6 us -> none  [tick_fn(): return (lax.ppermute(sent_rows, 'stage', fwd_perm), collect, cache_state)]
    unnamed x18 -> x6, local copies, waits for them, and re-layouts: 26.2 us -> 1.27 us
    dynamic_update_slice x8 -> x0, other arithmetic: 19.2 us -> none  [the longest x4 16.7 us: stage_fn(): lax.dynamic_update_slice(vd_all, vd_m[None, None], (layer_idx, micro_c, 0...]
    slice x20 -> x0, local copies, waits for them, and re-layouts: 15.2 us -> none  [the longest x8 6.3 us: keep_rows(): return jnp.concatenate([acts[:dec_rows], acts[-1:]], axis=0)]
  transfers between devices with their start and end apart: 12 -> 0, of which waited for: 12 -> 0; matrix products, arithmetic and copies ran while one was open for 0% -> 0% of each run, Pallas kernels for 0% -> 0%
where the time goes in v1:
time: 204 us; the launch traced here: 203 us
  Pallas kernels  199 us (98%)
  local copies, waits for them, and re-layouts  2.53 us (1%)
    pallas_call x1, Pallas kernels, device_fn(): pl.pallas_call(functools.partial(pipeline_kernel, n_stages), out_shape=(j...  169 us
    pallas_call x1, Pallas kernels, device_fn(): pl.pallas_call(cache_kernel, grid=(n_micro, dec_rows // n_seq), out_shape...  19.1 us
    pallas_call x1, Pallas kernels, device_fn(): pl.pallas_call(head_kernel, grid=(vocab // v_blk,), out_shape=jax.ShapeDt...  10.8 us

profile of v1, /device:TPU:113, one launch (start us, length us, event | category | flops | bytes accessed | tf_op | source)
XLA Modules:
  0.0 202.9 jit_solution(11728075999839590814)
XLA Ops:
  1.3 1.3 reshape.37.g_final
  2.5 169.2 %pipeline.1 = (bf16[4,40,896]{2,1,0:T(8,128)(2,1)}, bf16[4,32,128]{2,1,0:T(8,128)(2,1)}, bf16[4,32,128]{2,1,0:T(8,128)(2,1)}, bf16[128,256]{1,0:T(8,128)(2,1)}, bf16[128,256]{1,0:T(8,128)(2,1)}) custom-call(s32[4,32]{1,0:T(4,128)} %dec_len.3, s32[1]{0:T(128)S(6)} %copy.27.pre_len, f32[1,128]{1,0:T(1,128)} %constant.2.clone.inv_freq, bf16[1,896]{1,0:T(2,128)(2,1)} %g_attn.1, ...), custom_call_target="tpu_custom_call" | custom-call | tf_op jit(solution)/shard_map/pipeline/pallas_call | solution.py:393
  171.8 10.8 %head.1 = f32[33,4,8192]{2,1,0:T(4,128)} custom-call(bf16[4,40,896]{2,1,0:T(8,128)(2,1)} %get-tuple-element.12.fin, bf16[896,8192]{1,0:T(8,128)(2,1)} %w_head.1), custom_call_target="tpu_custom_call" | custom-call | tf_op jit(solution)/shard_map/head/pallas_call | solution.py:440
  182.5 0.0 copy-start.1
  182.5 0.0 copy-start
  182.5 19.1 %cache.1 = (bf16[4,32,128,256]{3,2,1,0:T(8,128)(2,1)}, bf16[4,32,128,256]{3,2,1,0:T(8,128)(2,1)}) custom-call(s32[4,32]{1,0:T(4,128)} %dec_len.3, bf16[4,32,128]{2,1,0:T(8,128)(2,1)} %get-tuple-element.13.kn, bf16[4,32,128]{2,1,0:T(8,128)(2,1)} %get-tuple-element.14.vn, bf16[4,32,128,256]{3,2,1,0:T(8,128)(2,1)} %bitcast.49, bf16[4,32,128,256]{3,2,1,0:T(8,128)(2,1)} %bitcast.51), custom_call_target="tpu_custom_call" | custom-call | tf_op jit(solution)/shard_map/cache/pallas_call | solution.py:456
  201.6 0.0 copy-done.1
  201.6 0.6 copy.28
  202.3 0.0 copy-done
  202.3 0.6 copy.29
Async XLA Ops:
  182.5 19.1 %copy-start.1 = (bf16[128,256]{1,0:T(8,128)(2,1)S(1)}, bf16[128,256]{1,0:T(8,128)(2,1)}, u32[]{:S(2)}) copy-start(bf16[128,256]{1,0:T(8,128)(2,1)} %get-tuple-element.17) | copy-start | bytes 196612
  182.5 19.7 %copy-start = (bf16[128,256]{1,0:T(8,128)(2,1)S(1)}, bf16[128,256]{1,0:T(8,128)(2,1)}, u32[]{:S(2)}) copy-start(bf16[128,256]{1,0:T(8,128)(2,1)} %get-tuple-element.18) | copy-start | bytes 196612

commit v2 on v1

--- a/solution.py
+++ b/solution.py
@@ -17,6 +17,7 @@
 VMEM = pltpu.VMEM
 SMEM = pltpu.SMEM
 MESH = pl.DeviceIdType.MESH
+JOIN = 2
 
 
 def rms_norm(acts, gain):
@@ -43,12 +44,13 @@
     dec_len, pre_len, inv_freq, g_attn, g_mlp, g_final,
     x_dec, x_pre, w_q, w_k, w_v, w_o, w_gate, w_up, w_down, k_dec, v_dec, k_pre, v_pre,
     fin_out, kn_out, vn_out, kp_out, vp_out,
-    wqkv, wo, w1, w3, w2, kc, vc, kp, vp, xin, xout, fin, qd, od, kn, vn, cosv, sinv, hid,
+    wqkv, wo, w1, w3, w2, kc, vc, kp, vp, xin, xout, fin, qd, od, kn, vn, cosv, sinv, hid, sp, pp, pd,
     w_sem, kv_sem, p_sem, x_sem, o_sem, send_sem, recv_sem, fsend_sem, frecv_sem,
 ):
     n_micro, n_rows, hidden = xin.shape
     dec_rows = x_dec.shape[1]
     seg_len = x_pre.shape[1]
+    per_micro = dec_len.shape[1]
     kv_width, cache_len = kp.shape
     q_width = wo.shape[0]
     ffn = w1.shape[1]
@@ -59,6 +61,7 @@
     stage = lax.axis_index('stage')
     last = n_stages - 1
     half = ffn // 2
+    seg_micro = seg_len * per_micro // dec_rows
 
     barrier = pltpu.get_barrier_semaphore()
 
@@ -68,11 +71,11 @@
             pltpu.make_async_copy(x_pre.at[m], xin.at[m, pl.ds(dec_rows, seg_len)], x_sem.at[m, 1]),
         )
 
-    def kv_copies(m):
-        return (
-            pltpu.make_async_copy(k_dec.at[m], kc.at[m], kv_sem.at[m, 0]),
-            pltpu.make_async_copy(v_dec.at[m], vc.at[m], kv_sem.at[m, 1]),
-        )
+    def k_copy(m):
+        return pltpu.make_async_copy(k_dec.at[m], kc.at[m], kv_sem.at[m, 0])
+
+    def v_copy(m):
+        return pltpu.make_async_copy(v_dec.at[m], vc.at[m], kv_sem.at[m, 1])
 
     qkv_copies = (
         pltpu.make_async_copy(w_q, wqkv.at[:, pl.ds(0, q_width)], w_sem.at[0]),
@@ -97,7 +100,7 @@
     def _():
         for copy in x_copies(0):
             copy.start()
-    for copy in qkv_copies + pre_copies + kv_copies(0) + wo_copies + up_copies[0] + up_copies[1] + down_copies:
+    for copy in qkv_copies + pre_copies + (k_copy(0), v_copy(0)) + wo_copies + up_copies[0] + up_copies[1] + down_copies:
         copy.start()
 
     @pl.when(stage == 0)
@@ -106,7 +109,7 @@
             for copy in x_copies(m):
                 copy.start()
     for m in range(1, n_micro):
-        for copy in kv_copies(m):
+        for copy in (k_copy(m), v_copy(m)):
             copy.start()
 
     @pl.when(stage > 0)
@@ -127,7 +130,7 @@
             if g < dec_rows // 8:
                 pos = jnp.zeros((8, 128), jnp.int32)
                 for r in range(8):
-                    pos = jnp.where(row8 == r, dec_len[m, g * 8 + r], pos)
+                    pos = jnp.where(row8 == r, dec_len[m * (dec_rows // per_micro) + (g * 8 + r) // per_micro, (g * 8 + r) % per_micro], pos)
             else:
                 pos = pre_len[0] + m * seg_len + (g * 8 - dec_rows) + row8
             angle = pos.astype(F32) * freq
@@ -217,26 +220,22 @@
 
         scale = head_dim ** -0.5
         pre_valid = seg_col <= seg_row + pre_begin
-        valid_g = jnp.concatenate([pre_valid] * group, axis=0)
-        pre_heads = []
+        span = group * seg_len
         for g in range(kv_count):
             rows = []
             for j in range(g * group, (g + 1) * group):
                 keep = low_half if j % 2 == 0 else jnp.logical_not(low_half)
                 rows.append(jnp.where(keep, q_tiles[j // 2][dec_rows:], 0.0).astype(BF16))
-            q_g = jnp.concatenate(rows, axis=0)
             k_g = kp_f[g * head_dim:(g + 1) * head_dim]
-            v_g = vp_f[g * head_dim:(g + 1) * head_dim]
-            scores = dot(q_g, jnp.concatenate([k_g, k_g], axis=0)) * scale
-            probs = softmax(jnp.where(valid_g, scores, NEG)).astype(BF16)
-            mixed = dot_t(probs, jnp.concatenate([v_g, v_g], axis=0))
-            pre_heads += [mixed[i * seg_len:(i + 1) * seg_len] for i in range(group)]
-
-        for copy in kv_copies(m):
-            copy.wait()
+            sp[g * span:(g + 1) * span, :] = dot(jnp.concatenate(rows, axis=0), jnp.concatenate([k_g, k_g], axis=0))
+        for j in range(q_heads):
+            scores = sp[j * seg_len:(j + 1) * seg_len, :] * scale
+            pp[j * seg_len:(j + 1) * seg_len, :] = softmax(jnp.where(pre_valid, scores, NEG)).astype(BF16)
+
+        k_copy(m).wait()
         pos_lane = lax.broadcasted_iota(jnp.int32, (16, cache_len), 1)
         for b in range(dec_rows):
-            pos = dec_len[m, b]
+            pos = dec_len[m * (dec_rows // per_micro) + b // per_micro, b % per_micro]
             q_b = qd[b * 16:(b + 1) * 16, :]
             s_old = dot(q_b.astype(BF16), kc[m, b]) * scale
             s_new = jnp.sum(q_b * kn[b:b + 1, :], axis=-1, keepdims=True) * scale
@@ -245,9 +244,18 @@
             peak = jnp.max(scores, axis=-1, keepdims=True)
             expd = jnp.exp(scores - peak)
             inv = 1.0 / jnp.sum(expd, axis=-1, keepdims=True)
-            p_old = jnp.where(here, 0.0, expd * inv).astype(BF16)
+            pd[b * 16:(b + 1) * 16, :] = jnp.where(here, 0.0, expd * inv).astype(BF16)
             p_new = (jnp.exp(s_new - peak) * inv).astype(BF16).astype(F32)
-            od[b * 16:(b + 1) * 16, :] = dot_t(p_old, vc[m, b]) + p_new * vn[b:b + 1, :]
+            od[b * 16:(b + 1) * 16, :] = p_new * vn[b:b + 1, :]
+
+        pre_heads = []
+        for g in range(kv_count):
+            v_g = vp_f[g * head_dim:(g + 1) * head_dim]
+            mixed = dot_t(pp[g * span:(g + 1) * span, :], jnp.concatenate([v_g, v_g], axis=0))
+            pre_heads += [mixed[i * seg_len:(i + 1) * seg_len] for i in range(group)]
+        v_copy(m).wait()
+        for b in range(dec_rows):
+            od[b * 16:(b + 1) * 16, :] += dot_t(pd[b * 16:(b + 1) * 16, :], vc[m, b])
 
         att_tiles = []
         for t in range(q_width // 128):
@@ -296,8 +304,9 @@
 
         @pl.when(stage == last)
         def _():
-            tail = jnp.concatenate([acts[:dec_rows], acts[n_rows - 8:]], axis=0)
-            fin[m] = rms_norm(tail, g_final[...])
+            ends = [acts[dec_rows + e - 8:dec_rows + e] for e in range(seg_micro, seg_len + 1, seg_micro)]
+            tail = jnp.concatenate([acts[:dec_rows]] + ends, axis=0)
+            fin[m] = rms_norm(tail, g_final[...].astype(F32)[None, :])
             for target in range(n_stages - 1):
                 fin_send(m, target).start()
         return carry
@@ -329,35 +338,62 @@
     fin_copy.wait()
 
 
-def head_kernel(fin, w_head, logits, rows):
-    n_micro = fin.shape[0]
+def head_kernel(micros, fin, w_head, logits, rows):
+    n_chunk, fin_rows, _ = fin.shape
     n_kept = logits.shape[0]
+    join = micros // n_chunk
 
     @pl.when(pl.program_id(0) == 0)
     def _():
-        for m in range(n_micro):
-            kept = fin[m].astype(F32)
+        for m in range(micros):
+            kept = fin[m // join].astype(F32)
+            first = (m % join) * (n_kept - 1)
+            last = (n_kept - 1) * join + 8 * (m % join) + 7
             for t in range(rows.shape[0]):
                 tile = kept[:, t * 128:(t + 1) * 128]
-                rows[t, pl.ds(m, n_kept - 1, stride=n_micro), :] = tile[:n_kept - 1]
-                rows[t, (n_kept - 1) * n_micro + m:(n_kept - 1) * n_micro + m + 1, :] = tile[fin.shape[1] - 1:]
+                rows[t, pl.ds(m, n_kept - 1, stride=micros), :] = tile[first:first + n_kept - 1]
+                rows[t, (n_kept - 1) * micros + m:(n_kept - 1) * micros + m + 1, :] = tile[last:last + 1]
 
     lhs = jnp.concatenate([rows[t].astype(BF16) for t in range(rows.shape[0])], axis=1)
     out = dot(lhs, w_head[...])
     for i in range(n_kept):
-        logits[i] = out[i * n_micro:(i + 1) * n_micro]
-
-
-def cache_kernel(dec_len, kn, vn, k_in, v_in, k_out, v_out):
-    n_seq, kv_width, cache_len = k_in.shape[1:]
-    m = pl.program_id(0)
-    first = pl.program_id(1) * n_seq
-    col = lax.broadcasted_iota(jnp.int32, (kv_width, cache_len), 1)
-    for new, old, out in ((kn, k_in, k_out), (vn, v_in, v_out)):
-        cols = jnp.transpose(new[0].astype(F32))
-        for b in range(n_seq):
-            here = col == dec_len[m, first + b]
-            out[0, b] = jnp.where(here, cols[:, b:b + 1], old[0, b].astype(F32)).astype(BF16)
+        logits[i] = out[i * micros:(i + 1) * micros]
+
+
+def cache_kernel(dec_len, kn, vn, k_in, v_in, k_out, v_out, buf, in_sem, out_sem):
+    n_slot, n_seq, kv_width, cache_len = buf.shape
+    n_chunk, dec_rows = k_in.shape[:2]
+    per_micro = dec_len.shape[1]
+    blocks = [(t, m, b) for m in range(n_chunk) for b in range(0, dec_rows, n_seq) for t in range(2)]
+    arrays = ((kn, k_in, k_out), (vn, v_in, v_out))
+
+    def load(i):
+        t, m, b = blocks[i]
+        return pltpu.make_async_copy(arrays[t][1].at[m, pl.ds(b, n_seq)], buf.at[i % n_slot], in_sem.at[i % n_slot])
+
+    def store(i):
+        t, m, b = blocks[i]
+        return pltpu.make_async_copy(buf.at[i % n_slot], arrays[t][2].at[m, pl.ds(b, n_seq)], out_sem.at[i % n_slot])
+
+    ahead = n_slot // 2
+    for i in range(ahead):
+        load(i).start()
+    lane = lax.broadcasted_iota(jnp.int32, (kv_width, 128), 1)
+    for i, (t, m, b) in enumerate(blocks):
+        if i + ahead < len(blocks):
+            if i + ahead >= n_slot:
+                store(i + ahead - n_slot).wait()
+            load(i + ahead).start()
+        load(i).wait()
+        cols = jnp.transpose(arrays[t][0][m, b:b + n_seq, :].astype(F32))
+        for r in range(n_seq):
+            pos = dec_len[m * (dec_rows // per_micro) + (b + r) // per_micro, (b + r) % per_micro]
+            at = pl.ds(pl.multiple_of(pos // 128 * 128, 128), 128)
+            old = buf[i % n_slot, r, :, at]
+            buf[i % n_slot, r, :, at] = jnp.where(lane == pos % 128, cols[:, r:r + 1], old.astype(F32)).astype(BF16)
+        store(i).start()
+    for i in range(len(blocks) - n_slot, len(blocks)):
+        store(i).wait()
 
 
 def solution(mesh):
@@ -369,15 +405,19 @@
     out_specs = (part_spec,) + (cache_spec,) * 4
 
     def device_fn(x_dec, x_pre, dec_len, pre_len, g_attn, w_q, w_k, w_v, w_o, g_mlp, w_gate, w_up, w_down, g_final, w_head, k_dec, v_dec, k_pre, v_pre):
-        n_micro, dec_rows, hidden = x_dec.shape
-        seg_len = x_pre.shape[1]
+        micros, micro_rows, hidden = x_dec.shape
+        n_micro = micros // JOIN
+        dec_rows = micro_rows * JOIN
+        seg_len = x_pre.shape[1] * JOIN
+        x_dec = x_dec.reshape(n_micro, dec_rows, hidden)
+        x_pre = x_pre.reshape(n_micro, seg_len, hidden)
         n_rows = dec_rows + seg_len
         _, cache_len, kv_count, head_dim = k_pre.shape
         kv_width = kv_count * head_dim
         q_width = w_q.shape[2]
         ffn = w_gate.shape[2]
         vocab = w_head.shape[1]
-        fin_rows = dec_rows + 8
+        fin_rows = dec_rows + 8 * JOIN
 
         kd = jnp.transpose(k_dec[0], (0, 1, 3, 4, 2)).reshape(n_micro, dec_rows, kv_width, cache_len)
         vd = jnp.transpose(v_dec[0], (0, 1, 3, 4, 2)).reshape(n_micro, dec_rows, kv_width, cache_len)
@@ -421,6 +461,9 @@
                 VMEM((n_micro, n_rows, 128), F32),
                 VMEM((n_micro, n_rows, 128), F32),
                 VMEM((n_rows, ffn), BF16),
+                VMEM((q_width // head_dim * seg_len, cache_len), F32),
+                VMEM((q_width // head_dim * seg_len, cache_len), BF16),
+                VMEM((dec_rows * 16, cache_len), BF16),
                 pltpu.SemaphoreType.DMA((9,)),
                 pltpu.SemaphoreType.DMA((n_micro, 2)),
                 pltpu.SemaphoreType.DMA((2,)),
@@ -433,37 +476,39 @@
             ],
             compiler_params=pltpu.CompilerParams(collective_id=0, has_side_effects=True, vmem_limit_bytes=62 * 1024 * 1024),
             name='pipeline',
-        )(dec_len, pre_len, inv_freq, g_attn, g_mlp, g_final.reshape(1, hidden),
+        )(dec_len, pre_len, inv_freq, g_attn, g_mlp, g_final,
           x_dec, x_pre, w_q[0], w_k[0], w_v[0], w_o[0], w_gate[0], w_up[0], w_down[0], kd, vd, kpre, vpre)
 
         v_blk = 1024
         logits = pl.pallas_call(
-            head_kernel,
+            functools.partial(head_kernel, micros),
             grid=(vocab // v_blk,),
-            out_shape=jax.ShapeDtypeStruct((dec_rows + 1, n_micro, vocab), F32),
+            out_shape=jax.ShapeDtypeStruct((micro_rows + 1, micros, vocab), F32),
             in_specs=[
                 pl.BlockSpec((n_micro, fin_rows, hidden), lambda n: (0, 0, 0)),
                 pl.BlockSpec((hidden, v_blk), lambda n: (0, n)),
             ],
-            out_specs=pl.BlockSpec((dec_rows + 1, n_micro, v_blk), lambda n: (0, 0, n)),
-            scratch_shapes=[VMEM((hidden // 128, (dec_rows + 1) * n_micro, 128), F32)],
+            out_specs=pl.BlockSpec((micro_rows + 1, micros, v_blk), lambda n: (0, 0, n)),
+            scratch_shapes=[VMEM((hidden // 128, (micro_rows + 1) * micros, 128), F32)],
             name='head',
         )(fin, w_head)
 
-        n_seq = 8
-        new_spec = pl.BlockSpec((1, n_seq, kv_width), lambda m, b: (m, b, 0))
-        cache_blk = pl.BlockSpec((1, n_seq, kv_width, cache_len), lambda m, b: (m, b, 0, 0))
         kd_out, vd_out = pl.pallas_call(
             cache_kernel,
-            grid=(n_micro, dec_rows // n_seq),
             out_shape=(jax.ShapeDtypeStruct(kd.shape, BF16),) * 2,
-            in_specs=[spec(SMEM), new_spec, new_spec, cache_blk, cache_blk],
-            out_specs=(cache_blk, cache_blk),
+            in_specs=[spec(SMEM), spec(VMEM), spec(VMEM), spec(HBM), spec(HBM)],
+            out_specs=(spec(HBM), spec(HBM)),
+            scratch_shapes=[
+                VMEM((16, 16, kv_width, cache_len), BF16),
+                pltpu.SemaphoreType.DMA((16,)),
+                pltpu.SemaphoreType.DMA((16,)),
+            ],
+            compiler_params=pltpu.CompilerParams(vmem_limit_bytes=62 * 1024 * 1024),
             name='cache',
         )(dec_len, kn, vn, kd, vd)
 
         def dec_cache(arr):
-            return jnp.transpose(arr.reshape(n_micro, dec_rows, kv_count, head_dim, cache_len), (0, 1, 4, 2, 3))[None]
+            return jnp.transpose(arr.reshape(micros, micro_rows, kv_count, head_dim, cache_len), (0, 1, 4, 2, 3))[None]
 
         def pre_cache(arr):
             return jnp.transpose(arr.reshape(kv_count, head_dim, cache_len), (2, 0, 1))[None]

time: 204 us -> 144 us (0.71)
  Pallas kernels: 199 us -> 140 us
    pallas_call x1, Pallas kernels: 169 us -> 116 us  [device_fn(): pl.pallas_call(functools.partial(pipeline_kernel, n_stages), out_shape=(j...]
    pallas_call x2, Pallas kernels: 29.8 us -> 23.9 us  [the longest x1 13.2 us: device_fn(): pl.pallas_call(cache_kernel, out_shape=(jax.ShapeDtypeStruct(kd.shape, BF...]
where the time goes in v2:
time: 144 us; the launch traced here: 142 us
  Pallas kernels  140 us (97%)
    pallas_call x1, Pallas kernels, device_fn(): pl.pallas_call(functools.partial(pipeline_kernel, n_stages), out_shape=(j...  116 us
    pallas_call x1, Pallas kernels, device_fn(): pl.pallas_call(cache_kernel, out_shape=(jax.ShapeDtypeStruct(kd.shape, BF...  13.2 us
    pallas_call x1, Pallas kernels, device_fn(): pl.pallas_call(functools.partial(head_kernel, micros), grid=(vocab // v_b...  10.8 us

profile of v2, /device:TPU:113, one launch (start us, length us, event | category | flops | bytes accessed | tf_op | source)
XLA Modules:
  0.0 142.4 jit_solution(12139276650923380666)
XLA Ops:
  1.3 115.9 %pipeline.1 = (bf16[2,80,896]{2,1,0:T(8,128)(2,1)}, bf16[2,64,128]{2,1,0:T(8,128)(2,1)}, bf16[2,64,128]{2,1,0:T(8,128)(2,1)}, bf16[128,256]{1,0:T(8,128)(2,1)}, bf16[128,256]{1,0:T(8,128)(2,1)}) custom-call(s32[4,32]{1,0:T(4,128)} %dec_len.3, s32[1]{0:T(128)S(6)} %copy.27.pre_len, f32[1,128]{1,0:T(1,128)} %constant.2.clone.inv_freq, bf16[1,896]{1,0:T(2,128)(2,1)} %g_attn.1, ...), custom_call_target="tpu_custom_call" | custom-call | tf_op jit(solution)/shard_map/pipeline/pallas_call | solution.py:433
  117.2 10.8 %head.1 = f32[33,4,8192]{2,1,0:T(4,128)} custom-call(bf16[2,80,896]{2,1,0:T(8,128)(2,1)} %get-tuple-element.12.fin, bf16[896,8192]{1,0:T(8,128)(2,1)} %w_head.1), custom_call_target="tpu_custom_call" | custom-call | tf_op jit(solution)/shard_map/head/pallas_call | solution.py:483
  128.0 0.0 copy-start.1
  128.0 0.0 copy-start
  128.0 13.2 %cache.1 = (bf16[2,64,128,256]{3,2,1,0:T(8,128)(2,1)}, bf16[2,64,128,256]{3,2,1,0:T(8,128)(2,1)}) custom-call(s32[4,32]{1,0:T(4,128)} %dec_len.3, bf16[2,64,128]{2,1,0:T(8,128)(2,1)} %get-tuple-element.13.kn, bf16[2,64,128]{2,1,0:T(8,128)(2,1)} %get-tuple-element.14.vn, bf16[2,64,128,256]{3,2,1,0:T(8,128)(2,1)} %bitcast.51, bf16[2,64,128,256]{3,2,1,0:T(8,128)(2,1)} %bitcast.53), custom_call_target="tpu_custom_call" | custom-call | tf_op jit(solution)/shard_map/cache/pallas_call | solution.py:496
  141.1 0.0 copy-done.1
  141.1 0.6 copy.28
  141.8 0.0 copy-done
  141.8 0.6 copy.29
Async XLA Ops:
  128.0 13.2 %copy-start.1 = (bf16[128,256]{1,0:T(8,128)(2,1)S(1)}, bf16[128,256]{1,0:T(8,128)(2,1)}, u32[]{:S(2)}) copy-start(bf16[128,256]{1,0:T(8,128)(2,1)} %get-tuple-element.17) | copy-start | bytes 196612
  128.0 13.8 %copy-start = (bf16[128,256]{1,0:T(8,128)(2,1)S(1)}, bf16[128,256]{1,0:T(8,128)(2,1)}, u32[]{:S(2)}) copy-start(bf16[128,256]{1,0:T(8,128)(2,1)} %get-tuple-element.18) | copy-start | bytes 196612

commit v3 on v2

--- a/solution.py
+++ b/solution.py
@@ -17,6 +17,7 @@
 VMEM = pltpu.VMEM
 SMEM = pltpu.SMEM
 MESH = pl.DeviceIdType.MESH
+R1_MB = 25
 JOIN = 2
 
 
@@ -41,11 +42,11 @@
 
 def pipeline_kernel(
     n_stages,
-    dec_len, pre_len, inv_freq, g_attn, g_mlp, g_final,
-    x_dec, x_pre, w_q, w_k, w_v, w_o, w_gate, w_up, w_down, k_dec, v_dec, k_pre, v_pre,
-    fin_out, kn_out, vn_out, kp_out, vp_out,
-    wqkv, wo, w1, w3, w2, kc, vc, kp, vp, xin, xout, fin, qd, od, kn, vn, cosv, sinv, hid, sp, pp, pd,
-    w_sem, kv_sem, p_sem, x_sem, o_sem, send_sem, recv_sem, fsend_sem, frecv_sem,
+    dec_len, pre_len, inv_freq_in, g_attn_in, g_mlp_in, g_final_in,
+    x_dec, x_pre, w_q, w_k, w_v, w_o, w_gate, w_up, w_down, k_dec, v_dec, k_pre, v_pre, w_head,
+    kc, vc, w1, fin_out, kp_out, vp_out,
+    inv_freq, g_attn, g_mlp, g_final, wqkv, wo, w3, w2, kp, vp, xin, fin, qd, kn, vn, cosv, sinv, hid, sp,
+    w_sem, kv_sem, p_sem, x_sem, o_sem, g_sem, send_sem, recv_sem, fsend_sem, frecv_sem,
 ):
     n_micro, n_rows, hidden = xin.shape
     dec_rows = x_dec.shape[1]
@@ -53,7 +54,7 @@
     per_micro = dec_len.shape[1]
     kv_width, cache_len = kp.shape
     q_width = wo.shape[0]
-    ffn = w1.shape[1]
+    ffn = w2.shape[0]
     head_dim = 64
     kv_count = kv_width // head_dim
     q_heads = q_width // head_dim
@@ -94,7 +95,13 @@
         )
         for i in range(2)
     )
+    head_copies = (pltpu.make_async_copy(w_head.at[:, pl.ds(0, ffn)], w1, w_sem.at[9]),)
     down_copies = (pltpu.make_async_copy(w_down, w2, w_sem.at[8]),)
+
+    gain_copies = [pltpu.make_async_copy(src, dst, g_sem.at[i]) for i, (src, dst) in enumerate((
+        (inv_freq_in, inv_freq), (g_attn_in, g_attn), (g_mlp_in, g_mlp), (g_final_in, g_final)))]
+    for copy in gain_copies:
+        copy.start()
 
     @pl.when(stage == 0)
     def _():
@@ -119,6 +126,9 @@
     @pl.when(stage < last)
     def _():
         pl.semaphore_signal(barrier, inc=1, device_id={'stage': last}, device_id_type=MESH)
+
+    for copy in gain_copies:
+        copy.wait()
 
     lane = lax.broadcasted_iota(jnp.int32, (8, 128), 1)
     row8 = lax.broadcasted_iota(jnp.int32, (8, 128), 0)
@@ -151,7 +161,7 @@
 
     def x_send(m):
         return pltpu.make_async_remote_copy(
-            src_ref=xout.at[m], dst_ref=xin.at[m], send_sem=send_sem.at[m], recv_sem=recv_sem.at[m],
+            src_ref=xin.at[m], dst_ref=xin.at[m], send_sem=send_sem.at[m], recv_sem=recv_sem.at[m],
             device_id={'stage': jnp.minimum(stage + 1, last)}, device_id_type=MESH)
 
     def fin_send(m, target):
@@ -192,10 +202,8 @@
         q_tiles = [rotate(proj[:, t * 128:(t + 1) * 128]).astype(BF16).astype(F32) for t in range(q_width // 128)]
         k_new = rotate(proj[:, q_width:q_width + kv_width]).astype(BF16)
         v_new = proj[:, q_width + kv_width:].astype(BF16)
-        kn[...] = k_new[:dec_rows].astype(F32)
-        vn[...] = v_new[:dec_rows].astype(F32)
-        kn_out[m] = k_new[:dec_rows]
-        vn_out[m] = v_new[:dec_rows]
+        kn[m] = k_new[:dec_rows].astype(F32)
+        vn[m] = v_new[:dec_rows].astype(F32)
 
         for j in range(q_heads):
             tile = q_tiles[j // 2][:dec_rows]
@@ -221,16 +229,18 @@
         scale = head_dim ** -0.5
         pre_valid = seg_col <= seg_row + pre_begin
         span = group * seg_len
+        pd_base = q_heads * seg_len
         for g in range(kv_count):
             rows = []
             for j in range(g * group, (g + 1) * group):
                 keep = low_half if j % 2 == 0 else jnp.logical_not(low_half)
                 rows.append(jnp.where(keep, q_tiles[j // 2][dec_rows:], 0.0).astype(BF16))
             k_g = kp_f[g * head_dim:(g + 1) * head_dim]
-            sp[g * span:(g + 1) * span, :] = dot(jnp.concatenate(rows, axis=0), jnp.concatenate([k_g, k_g], axis=0))
-        for j in range(q_heads):
-            scores = sp[j * seg_len:(j + 1) * seg_len, :] * scale
-            pp[j * seg_len:(j + 1) * seg_len, :] = softmax(jnp.where(pre_valid, scores, NEG)).astype(BF16)
+            sp[...] = dot(jnp.concatenate(rows, axis=0), jnp.concatenate([k_g, k_g], axis=0))
+            for j in range(group):
+                scores = sp[j * seg_len:(j + 1) * seg_len, :] * scale
+                base = (g * group + j) * seg_len
+                hid[base:base + seg_len, :] = softmax(jnp.where(pre_valid, scores, NEG)).astype(BF16)
 
         k_copy(m).wait()
         pos_lane = lax.broadcasted_iota(jnp.int32, (16, cache_len), 1)
@@ -238,30 +248,30 @@
             pos = dec_len[m * (dec_rows // per_micro) + b // per_micro, b % per_micro]
             q_b = qd[b * 16:(b + 1) * 16, :]
             s_old = dot(q_b.astype(BF16), kc[m, b]) * scale
-            s_new = jnp.sum(q_b * kn[b:b + 1, :], axis=-1, keepdims=True) * scale
+            s_new = jnp.sum(q_b * kn[m, b:b + 1, :], axis=-1, keepdims=True) * scale
             here = pos_lane == pos
             scores = jnp.where(here, s_new, jnp.where(pos_lane < pos, s_old, NEG))
             peak = jnp.max(scores, axis=-1, keepdims=True)
             expd = jnp.exp(scores - peak)
             inv = 1.0 / jnp.sum(expd, axis=-1, keepdims=True)
-            pd[b * 16:(b + 1) * 16, :] = jnp.where(here, 0.0, expd * inv).astype(BF16)
+            hid[pd_base + b * 16:pd_base + (b + 1) * 16, :] = jnp.where(here, 0.0, expd * inv).astype(BF16)
             p_new = (jnp.exp(s_new - peak) * inv).astype(BF16).astype(F32)
-            od[b * 16:(b + 1) * 16, :] = p_new * vn[b:b + 1, :]
+            qd[b * 16:(b + 1) * 16, :] = p_new * vn[m, b:b + 1, :]
 
         pre_heads = []
         for g in range(kv_count):
             v_g = vp_f[g * head_dim:(g + 1) * head_dim]
-            mixed = dot_t(pp[g * span:(g + 1) * span, :], jnp.concatenate([v_g, v_g], axis=0))
+            mixed = dot_t(hid[g * span:(g + 1) * span, :], jnp.concatenate([v_g, v_g], axis=0))
             pre_heads += [mixed[i * seg_len:(i + 1) * seg_len] for i in range(group)]
         v_copy(m).wait()
         for b in range(dec_rows):
-            od[b * 16:(b + 1) * 16, :] += dot_t(pd[b * 16:(b + 1) * 16, :], vc[m, b])
+            qd[b * 16:(b + 1) * 16, :] += dot_t(hid[pd_base + b * 16:pd_base + (b + 1) * 16, :], vc[m, b])
 
         att_tiles = []
         for t in range(q_width // 128):
             parts = []
             for j in (2 * t, 2 * t + 1):
-                part = od[pl.ds(j, dec_rows, stride=16), :]
+                part = qd[pl.ds(j, dec_rows, stride=16), :]
                 if j % 2 != j // group:
                     part = pltpu.roll(part, head_dim, 1)
                 parts.append(part)
@@ -289,17 +299,25 @@
             for n in range(lo, hi, n_blk):
                 gate = dot(normed, w1[:, n:n + n_blk])
                 up = dot(normed, w3[:, n:n + n_blk])
-                hid[:, n:n + n_blk] = (jax.nn.silu(gate) * up).astype(BF16)
+                k = n // n_blk
+                hid[k * n_rows:(k + 1) * n_rows, :] = (jax.nn.silu(gate) * up).astype(BF16)
 
         @pl.when(first)
         def _():
             for copy in down_copies:
                 copy.wait()
-        acts = (acts.astype(F32) + dot(hid[...], w2[...])).astype(BF16)
+
+        @pl.when(m == n_micro - 1)
+        def _():
+            for copy in head_copies:
+                copy.start()
+
+        hidden_act = jnp.concatenate([hid[k * n_rows:(k + 1) * n_rows, :] for k in range(ffn // n_blk)], axis=1)
+        acts = (acts.astype(F32) + dot(hidden_act, w2[...])).astype(BF16)
 
         @pl.when(stage < last)
         def _():
-            xout[m] = acts
+            xin[m] = acts
             x_send(m).start()
 
         @pl.when(stage == last)
@@ -313,10 +331,22 @@
 
     lax.fori_loop(0, n_micro, tick, 0)
 
-    kp_copy = pltpu.make_async_copy(kp, kp_out, o_sem.at[0])
-    vp_copy = pltpu.make_async_copy(vp, vp_out, o_sem.at[1])
-    kp_copy.start()
-    vp_copy.start()
+    pre_out = (pltpu.make_async_copy(kp, kp_out, o_sem.at[0]), pltpu.make_async_copy(vp, vp_out, o_sem.at[1]))
+    for copy in pre_out:
+        copy.start()
+
+    col_full = lax.broadcasted_iota(jnp.int32, (kv_width, cache_len), 1)
+
+    def patch(m, carry):
+        for new, cache in ((kn, kc), (vn, vc)):
+            cols = jnp.transpose(new[m])
+            for b in range(dec_rows):
+                pos = dec_len[m * (dec_rows // per_micro) + b // per_micro, b % per_micro]
+                column = jnp.broadcast_to(cols[:, b:b + 1], (kv_width, cache_len)).astype(BF16)
+                cache[m, b] = jnp.where(col_full == pos, column, cache[m, b])
+        return carry
+
+    lax.fori_loop(0, n_micro, patch, 0)
 
     @pl.when(stage < last)
     def _():
@@ -333,67 +363,60 @@
 
     fin_copy = pltpu.make_async_copy(fin, fin_out, o_sem.at[2])
     fin_copy.start()
-    kp_copy.wait()
-    vp_copy.wait()
+    for copy in pre_out:
+        copy.wait()
     fin_copy.wait()
-
-
-def head_kernel(micros, fin, w_head, logits, rows):
-    n_chunk, fin_rows, _ = fin.shape
+    for copy in head_copies:
+        copy.wait()
+
+
+def output_kernel(micros, vocab, kc, vc, w_low, w_all, fin_in, kp_in, vp_in, logits, kc_out, vc_out, kp_out, vp_out, w_high, fin, kp, vp, rows, stage_buf, i_sem, c_sem, l_sem):
+    n_chunk = fin.shape[0]
     n_kept = logits.shape[0]
     join = micros // n_chunk
-
-    @pl.when(pl.program_id(0) == 0)
-    def _():
-        for m in range(micros):
-            kept = fin[m // join].astype(F32)
-            first = (m % join) * (n_kept - 1)
-            last = (n_kept - 1) * join + 8 * (m % join) + 7
-            for t in range(rows.shape[0]):
-                tile = kept[:, t * 128:(t + 1) * 128]
-                rows[t, pl.ds(m, n_kept - 1, stride=micros), :] = tile[first:first + n_kept - 1]
-                rows[t, (n_kept - 1) * micros + m:(n_kept - 1) * micros + m + 1, :] = tile[last:last + 1]
-
+    n_slot, _, _, v_blk = stage_buf.shape
+    copies = [pltpu.make_async_copy(src, dst, c_sem.at[i]) for i, (src, dst) in enumerate(((kc, kc_out), (vc, vc_out), (kp, kp_out), (vp, vp_out)))]
+    loads = [pltpu.make_async_copy(src, dst, i_sem.at[i]) for i, (src, dst) in enumerate(((fin_in, fin), (kp_in, kp), (vp_in, vp)))]
+    low = w_low.shape[1]
+    w_load = pltpu.make_async_copy(w_all.at[:, pl.ds(low, vocab - low)], w_high, i_sem.at[3])
+    for copy in loads + [w_load] + copies[:2]:
+        copy.start()
+    for copy in loads:
+        copy.wait()
+    for copy in copies[2:]:
+        copy.start()
+
+    for m in range(micros):
+        kept = fin[m // join].astype(F32)
+        first = (m % join) * (n_kept - 1)
+        last = (n_kept - 1) * join + 8 * (m % join) + 7
+        for t in range(rows.shape[0]):
+            tile = kept[:, t * 128:(t + 1) * 128]
+            rows[t, pl.ds(m, n_kept - 1, stride=micros), :] = tile[first:first + n_kept - 1]
+            rows[t, (n_kept - 1) * micros + m:(n_kept - 1) * micros + m + 1, :] = tile[last:last + 1]
     lhs = jnp.concatenate([rows[t].astype(BF16) for t in range(rows.shape[0])], axis=1)
-    out = dot(lhs, w_head[...])
-    for i in range(n_kept):
-        logits[i] = out[i * micros:(i + 1) * micros]
-
-
-def cache_kernel(dec_len, kn, vn, k_in, v_in, k_out, v_out, buf, in_sem, out_sem):
-    n_slot, n_seq, kv_width, cache_len = buf.shape
-    n_chunk, dec_rows = k_in.shape[:2]
-    per_micro = dec_len.shape[1]
-    blocks = [(t, m, b) for m in range(n_chunk) for b in range(0, dec_rows, n_seq) for t in range(2)]
-    arrays = ((kn, k_in, k_out), (vn, v_in, v_out))
-
-    def load(i):
-        t, m, b = blocks[i]
-        return pltpu.make_async_copy(arrays[t][1].at[m, pl.ds(b, n_seq)], buf.at[i % n_slot], in_sem.at[i % n_slot])
+
+    blocks = [(w_low, 0, n, min(v_blk, low - n)) for n in range(0, low, v_blk)]
+    blocks += [(w_high, low, n, min(v_blk, vocab - low - n)) for n in range(0, vocab - low, v_blk)]
 
     def store(i):
-        t, m, b = blocks[i]
-        return pltpu.make_async_copy(buf.at[i % n_slot], arrays[t][2].at[m, pl.ds(b, n_seq)], out_sem.at[i % n_slot])
-
-    ahead = n_slot // 2
-    for i in range(ahead):
-        load(i).start()
-    lane = lax.broadcasted_iota(jnp.int32, (kv_width, 128), 1)
-    for i, (t, m, b) in enumerate(blocks):
-        if i + ahead < len(blocks):
-            if i + ahead >= n_slot:
-                store(i + ahead - n_slot).wait()
-            load(i + ahead).start()
-        load(i).wait()
-        cols = jnp.transpose(arrays[t][0][m, b:b + n_seq, :].astype(F32))
-        for r in range(n_seq):
-            pos = dec_len[m * (dec_rows // per_micro) + (b + r) // per_micro, (b + r) % per_micro]
-            at = pl.ds(pl.multiple_of(pos // 128 * 128, 128), 128)
-            old = buf[i % n_slot, r, :, at]
-            buf[i % n_slot, r, :, at] = jnp.where(lane == pos % 128, cols[:, r:r + 1], old.astype(F32)).astype(BF16)
+        _, base, n, width = blocks[i]
+        return pltpu.make_async_copy(
+            stage_buf.at[i % n_slot, :, :, pl.ds(0, width)], logits.at[:, :, pl.ds(base + n, width)], l_sem.at[i % n_slot])
+
+    for i, (w_ref, base, n, width) in enumerate(blocks):
+        if i >= n_slot:
+            store(i - n_slot).wait()
+        if base and n == 0:
+            w_load.wait()
+        out = dot(lhs, w_ref[:, n:n + width])
+        for r in range(n_kept):
+            stage_buf[i % n_slot, r, :, :width] = out[r * micros:(r + 1) * micros]
         store(i).start()
     for i in range(len(blocks) - n_slot, len(blocks)):
         store(i).wait()
+    for copy in copies:
+        copy.wait()
 
 
 def solution(mesh):
@@ -430,82 +453,81 @@
         def spec(space):
             return pl.BlockSpec(memory_space=space)
 
-        fin, kn, vn, kp, vp = pl.pallas_call(
+        kc, vc, w1, fin, kp, vp = pl.pallas_call(
             functools.partial(pipeline_kernel, n_stages),
             out_shape=(
+                VMEM((n_micro, dec_rows, kv_width, cache_len), BF16),
+                VMEM((n_micro, dec_rows, kv_width, cache_len), BF16),
+                VMEM((hidden, ffn), BF16),
                 jax.ShapeDtypeStruct((n_micro, fin_rows, hidden), BF16),
-                jax.ShapeDtypeStruct((n_micro, dec_rows, kv_width), BF16),
-                jax.ShapeDtypeStruct((n_micro, dec_rows, kv_width), BF16),
                 jax.ShapeDtypeStruct((kv_width, cache_len), BF16),
                 jax.ShapeDtypeStruct((kv_width, cache_len), BF16),
             ),
-            in_specs=[spec(SMEM)] * 2 + [spec(VMEM)] * 4 + [spec(HBM)] * 13,
-            out_specs=(spec(HBM), spec(VMEM), spec(VMEM), spec(HBM), spec(HBM)),
+            in_specs=[spec(SMEM)] * 2 + [spec(HBM)] * 18,
+            out_specs=(spec(VMEM),) * 3 + (spec(HBM),) * 3,
             scratch_shapes=[
+                VMEM((1, 128), F32),
+                VMEM((1, hidden), BF16),
+                VMEM((1, hidden), BF16),
+                VMEM((hidden,), BF16),
                 VMEM((hidden, q_width + 2 * kv_width), BF16),
                 VMEM((q_width, hidden), BF16),
                 VMEM((hidden, ffn), BF16),
-                VMEM((hidden, ffn), BF16),
                 VMEM((ffn, hidden), BF16),
-                VMEM((n_micro, dec_rows, kv_width, cache_len), BF16),
-                VMEM((n_micro, dec_rows, kv_width, cache_len), BF16),
                 VMEM((kv_width, cache_len), BF16),
                 VMEM((kv_width, cache_len), BF16),
                 VMEM((n_micro, n_rows, hidden), BF16),
-                VMEM((n_micro, n_rows, hidden), BF16),
                 VMEM((n_micro, fin_rows, hidden), BF16),
                 VMEM((dec_rows * 16, 128), F32),
-                VMEM((dec_rows * 16, 128), F32),
-                VMEM((dec_rows, kv_width), F32),
-                VMEM((dec_rows, kv_width), F32),
+                VMEM((n_micro, dec_rows, kv_width), F32),
+                VMEM((n_micro, dec_rows, kv_width), F32),
                 VMEM((n_micro, n_rows, 128), F32),
                 VMEM((n_micro, n_rows, 128), F32),
-                VMEM((n_rows, ffn), BF16),
-                VMEM((q_width // head_dim * seg_len, cache_len), F32),
-                VMEM((q_width // head_dim * seg_len, cache_len), BF16),
-                VMEM((dec_rows * 16, cache_len), BF16),
-                pltpu.SemaphoreType.DMA((9,)),
+                VMEM((ffn // 256 * n_rows, 256), BF16),
+                VMEM((q_width // head_dim // kv_count * seg_len, cache_len), F32),
+                pltpu.SemaphoreType.DMA((10,)),
                 pltpu.SemaphoreType.DMA((n_micro, 2)),
                 pltpu.SemaphoreType.DMA((2,)),
                 pltpu.SemaphoreType.DMA((n_micro, 2)),
                 pltpu.SemaphoreType.DMA((3,)),
+                pltpu.SemaphoreType.DMA((4,)),
                 pltpu.SemaphoreType.DMA((n_micro,)),
                 pltpu.SemaphoreType.DMA((n_micro,)),
                 pltpu.SemaphoreType.DMA((n_micro, n_stages - 1)),
                 pltpu.SemaphoreType.DMA((n_micro,)),
             ],
-            compiler_params=pltpu.CompilerParams(collective_id=0, has_side_effects=True, vmem_limit_bytes=62 * 1024 * 1024),
+            compiler_params=pltpu.CompilerParams(collective_id=0, has_side_effects=True, vmem_limit_bytes=int(R1_MB * 1024 * 1024)),
             name='pipeline',
-        )(dec_len, pre_len, inv_freq, g_attn, g_mlp, g_final,
-          x_dec, x_pre, w_q[0], w_k[0], w_v[0], w_o[0], w_gate[0], w_up[0], w_down[0], kd, vd, kpre, vpre)
-
-        v_blk = 1024
-        logits = pl.pallas_call(
-            functools.partial(head_kernel, micros),
-            grid=(vocab // v_blk,),
-            out_shape=jax.ShapeDtypeStruct((micro_rows + 1, micros, vocab), F32),
-            in_specs=[
-                pl.BlockSpec((n_micro, fin_rows, hidden), lambda n: (0, 0, 0)),
-                pl.BlockSpec((hidden, v_blk), lambda n: (0, n)),
+        )(dec_len, pre_len, *(pltpu.with_memory_space_constraint(arr, pltpu.HBM) for arr in (
+              inv_freq, g_attn, g_mlp, g_final, x_dec, x_pre, w_q[0], w_k[0], w_v[0], w_o[0], w_gate[0], w_up[0], w_down[0], kd, vd, kpre, vpre, w_head)))
+
+        v_blk = 512
+        n_slot = 4
+        logits, kd_out, vd_out, kp_out, vp_out = pl.pallas_call(
+            functools.partial(output_kernel, micros, vocab),
+            out_shape=(
+                jax.ShapeDtypeStruct((micro_rows + 1, micros, vocab), F32),
+                jax.ShapeDtypeStruct(kd.shape, BF16),
+                jax.ShapeDtypeStruct(vd.shape, BF16),
+                jax.ShapeDtypeStruct(kpre.shape, BF16),
+                jax.ShapeDtypeStruct(vpre.shape, BF16),
+            ),
+            in_specs=[spec(VMEM)] * 3 + [spec(HBM)] * 4,
+            out_specs=(spec(HBM),) * 5,
+            scratch_shapes=[
+                VMEM((hidden, vocab - ffn), BF16),
+                VMEM((n_micro, fin_rows, hidden), BF16),
+                VMEM((kv_width, cache_len), BF16),
+                VMEM((kv_width, cache_len), BF16),
+                VMEM((hidden // 128, (micro_rows + 1) * micros, 128), F32),
+                VMEM((n_slot, micro_rows + 1, micros, v_blk), F32),
+                pltpu.SemaphoreType.DMA((4,)),
+                pltpu.SemaphoreType.DMA((4,)),
+                pltpu.SemaphoreType.DMA((n_slot,)),
             ],
-            out_specs=pl.BlockSpec((micro_rows + 1, micros, v_blk), lambda n: (0, 0, n)),
-            scratch_shapes=[VMEM((hidden // 128, (micro_rows + 1) * micros, 128), F32)],
-            name='head',
-        )(fin, w_head)
-
-        kd_out, vd_out = pl.pallas_call(
-            cache_kernel,
-            out_shape=(jax.ShapeDtypeStruct(kd.shape, BF16),) * 2,
-            in_specs=[spec(SMEM), spec(VMEM), spec(VMEM), spec(HBM), spec(HBM)],
-            out_specs=(spec(HBM), spec(HBM)),
-            scratch_shapes=[
-                VMEM((16, 16, kv_width, cache_len), BF16),
-                pltpu.SemaphoreType.DMA((16,)),
-                pltpu.SemaphoreType.DMA((16,)),
-            ],
-            compiler_params=pltpu.CompilerParams(vmem_limit_bytes=62 * 1024 * 1024),
-            name='cache',
-        )(dec_len, kn, vn, kd, vd)
+            compiler_params=pltpu.CompilerParams(vmem_limit_bytes=13 * 1024 * 1024),
+            name='output',
+        )(kc, vc, w1, pltpu.with_memory_space_constraint(w_head, pltpu.HBM), fin, kp, vp)
 
         def dec_cache(arr):
             return jnp.transpose(arr.reshape(micros, micro_rows, kv_count, head_dim, cache_len), (0, 1, 4, 2, 3))[None]
@@ -513,6 +535,6 @@
         def pre_cache(arr):
             return jnp.transpose(arr.reshape(kv_count, head_dim, cache_len), (2, 0, 1))[None]
 
-        return jnp.transpose(logits, (1, 0, 2)), dec_cache(kd_out), dec_cache(vd_out), pre_cache(kp), pre_cache(vp)
+        return jnp.transpose(logits, (1, 0, 2)), dec_cache(kd_out), dec_cache(vd_out), pre_cache(kp_out), pre_cache(vp_out)
 
     return jax.shard_map(device_fn, mesh=mesh, in_specs=in_specs, out_specs=out_specs, check_vma=False)

time: 144 us -> 134 us (0.931)
  Pallas kernels: 140 us -> 131 us
    pallas_call x3 -> x2, Pallas kernels: 140 us -> 131 us  [the longest x1 118 us: device_fn(): pl.pallas_call(functools.partial(pipeline_kernel, n_stages), out_shape=(V...]
where the time goes in v3:
time: 134 us; the launch traced here: 133 us
  Pallas kernels  131 us (98%)
  between operations  1.46 us (1%)
    pallas_call x1, Pallas kernels, device_fn(): pl.pallas_call(functools.partial(pipeline_kernel, n_stages), out_shape=(V...  118 us
    pallas_call x1, Pallas kernels, device_fn(): pl.pallas_call(functools.partial(output_kernel, micros, vocab), out_shape...  12.9 us

profile of v3, /device:TPU:113, one launch (start us, length us, event | category | flops | bytes accessed | tf_op | source)
XLA Modules:
  0.0 132.8 jit_solution(15822671915276590581)
XLA Ops:
  1.3 0.0 copy-start
  1.3 0.7 copy-done
  2.0 117.8 %pipeline.1 = (bf16[2,64,128,256]{3,2,1,0:T(8,128)(2,1)S(1)}, bf16[2,64,128,256]{3,2,1,0:T(8,128)(2,1)S(1)}, bf16[896,4864]{1,0:T(8,128)(2,1)S(1)}, bf16[2,80,89...) custom-call(s32[4,32]{1,0:T(4,128)S(1)} %copy-done, s32[1]{0:T(128)S(6)} %copy.25.pre_len, ...), custom_call_target="tpu_custom_call" | custom-call | tf_op jit(solution)/shard_map/pipeline/pallas_call | solution.py:456
  119.8 12.9 %output.1 = (f32[33,4,8192]{2,1,0:T(4,128)}, bf16[2,64,128,256]{3,2,1,0:T(8,128)(2,1)}, bf16[2,64,128,256]{3,2,1,0:T(8,128)(2,1)}, bf16[128,256]{1,0:T(8,128)(2,1)}, bf16[128,256]{1,0:T(8,128)(2,1)}) custom-call(bf16[2,64,128,256]{3,2,1,0:T(8,128)(2,1)S(1)} %get-tuple-element.16.kc, bf16[2,64,128,256]{3,2,1,0:T(8,128)(2,1)S(1)} %get-tuple-element.17.vc, ...), custom_call_target="tpu_custom_call" | custom-call | tf_op jit(solution)/shard_map/output/pallas_call | solution.py:506
Async XLA Ops:
  1.3 0.7 copy-start

commit v4 on v3

--- a/solution.py
+++ b/solution.py
@@ -17,7 +17,7 @@
 VMEM = pltpu.VMEM
 SMEM = pltpu.SMEM
 MESH = pl.DeviceIdType.MESH
-R1_MB = 25
+R1_MB = 26
 JOIN = 2
 
 
@@ -46,7 +46,7 @@
     x_dec, x_pre, w_q, w_k, w_v, w_o, w_gate, w_up, w_down, k_dec, v_dec, k_pre, v_pre, w_head,
     kc, vc, w1, fin_out, kp_out, vp_out,
     inv_freq, g_attn, g_mlp, g_final, wqkv, wo, w3, w2, kp, vp, xin, fin, qd, kn, vn, cosv, sinv, hid, sp,
-    w_sem, kv_sem, p_sem, x_sem, o_sem, g_sem, send_sem, recv_sem, fsend_sem, frecv_sem,
+    w_sem, kv_sem, p_sem, x_sem, o_sem, g_sem, send_sem, recv_sem, fsend_sem, frecv_sem, fnext_sem,
 ):
     n_micro, n_rows, hidden = xin.shape
     dec_rows = x_dec.shape[1]
@@ -123,7 +123,15 @@
     def _():
         pl.semaphore_signal(barrier, inc=1, device_id={'stage': stage - 1}, device_id_type=MESH)
 
-    @pl.when(stage < last)
+    fin_first = [last - 1] + list(range(last - 2, 0, -2))
+    passes_on = (stage % 2 == 1) & (stage < last)
+    ends_chain = (stage % 2 == 0) & (stage < last - 1)
+
+    @pl.when(ends_chain)
+    def _():
+        pl.semaphore_signal(barrier, inc=1, device_id={'stage': stage + 1}, device_id_type=MESH)
+
+    @pl.when((stage < last) & jnp.logical_not(ends_chain))
     def _():
         pl.semaphore_signal(barrier, inc=1, device_id={'stage': last}, device_id_type=MESH)
 
@@ -151,13 +159,17 @@
     lax.fori_loop(0, n_micro, table_body, 0)
     qd[...] = jnp.zeros(qd.shape, F32)
 
-    @pl.when(stage < last)
+    @pl.when((stage < last) & jnp.logical_not(passes_on))
     def _():
         pl.semaphore_wait(barrier, 1)
 
+    @pl.when(passes_on)
+    def _():
+        pl.semaphore_wait(barrier, 2)
+
     @pl.when(stage == last)
     def _():
-        pl.semaphore_wait(barrier, n_stages - 1)
+        pl.semaphore_wait(barrier, len(fin_first))
 
     def x_send(m):
         return pltpu.make_async_remote_copy(
@@ -169,22 +181,20 @@
             src_ref=fin.at[m], dst_ref=fin.at[m], send_sem=fsend_sem.at[m, target], recv_sem=frecv_sem.at[m],
             device_id={'stage': target}, device_id_type=MESH)
 
-    def tick(m, carry):
-        first = m == 0
-
-        @pl.when(stage == 0)
-        def _():
+    def tick(loading, m, carry):
+        def wait_first(copies):
+            if loading:
+                @pl.when(m == 0)
+                def _():
+                    for copy in copies:
+                        copy.wait()
+
+        if loading:
             for copy in x_copies(m):
                 copy.wait()
-
-        @pl.when(stage > 0)
-        def _():
+        else:
             x_send(m).wait_recv()
-
-        @pl.when(first)
-        def _():
-            for copy in qkv_copies + pre_copies:
-                copy.wait()
+        wait_first(qkv_copies + pre_copies)
 
         acts = xin[m]
         normed = rms_norm(acts, g_attn[...])
@@ -242,7 +252,8 @@
                 base = (g * group + j) * seg_len
                 hid[base:base + seg_len, :] = softmax(jnp.where(pre_valid, scores, NEG)).astype(BF16)
 
-        k_copy(m).wait()
+        if loading:
+            k_copy(m).wait()
         pos_lane = lax.broadcasted_iota(jnp.int32, (16, cache_len), 1)
         for b in range(dec_rows):
             pos = dec_len[m * (dec_rows // per_micro) + b // per_micro, b % per_micro]
@@ -263,7 +274,8 @@
             v_g = vp_f[g * head_dim:(g + 1) * head_dim]
             mixed = dot_t(hid[g * span:(g + 1) * span, :], jnp.concatenate([v_g, v_g], axis=0))
             pre_heads += [mixed[i * seg_len:(i + 1) * seg_len] for i in range(group)]
-        v_copy(m).wait()
+        if loading:
+            v_copy(m).wait()
         for b in range(dec_rows):
             qd[b * 16:(b + 1) * 16, :] += dot_t(hid[pd_base + b * 16:pd_base + (b + 1) * 16, :], vc[m, b])
 
@@ -280,20 +292,14 @@
             att_tiles.append(jnp.concatenate([dec_tile, pre_tile], axis=0).astype(BF16))
         att = jnp.concatenate(att_tiles, axis=1)
 
-        @pl.when(first)
-        def _():
-            for copy in wo_copies:
-                copy.wait()
+        wait_first(wo_copies)
 
         acts = (acts.astype(F32) + dot(att, wo[...])).astype(BF16)
         normed = rms_norm(acts, g_mlp[...])
 
         n_blk = 256
         for i in range(2):
-            @pl.when(first)
-            def _():
-                for copy in up_copies[i]:
-                    copy.wait()
+            wait_first(up_copies[i])
             lo = 0 if i == 0 else half // n_blk * n_blk
             hi = half // n_blk * n_blk if i == 0 else ffn
             for n in range(lo, hi, n_blk):
@@ -302,34 +308,48 @@
                 k = n // n_blk
                 hid[k * n_rows:(k + 1) * n_rows, :] = (jax.nn.silu(gate) * up).astype(BF16)
 
-        @pl.when(first)
-        def _():
-            for copy in down_copies:
-                copy.wait()
-
-        @pl.when(m == n_micro - 1)
-        def _():
-            for copy in head_copies:
-                copy.start()
-
+        wait_first(down_copies)
         hidden_act = jnp.concatenate([hid[k * n_rows:(k + 1) * n_rows, :] for k in range(ffn // n_blk)], axis=1)
         acts = (acts.astype(F32) + dot(hidden_act, w2[...])).astype(BF16)
 
-        @pl.when(stage < last)
-        def _():
+        def send_rows():
             xin[m] = acts
             x_send(m).start()
 
-        @pl.when(stage == last)
-        def _():
-            ends = [acts[dec_rows + e - 8:dec_rows + e] for e in range(seg_micro, seg_len + 1, seg_micro)]
-            tail = jnp.concatenate([acts[:dec_rows]] + ends, axis=0)
+        def send_final():
+            ends = [acts[dec_rows + e - 8:dec_rows + e].astype(F32) for e in range(seg_micro, seg_len + 1, seg_micro)]
+            row = lax.broadcasted_iota(jnp.int32, (8, hidden), 0)
+            kept = ends[-1]
+            for i, rows in enumerate(ends[:-1]):
+                shift = len(ends) - 1 - i
+                kept = jnp.where(row == 7 - shift, pltpu.roll(rows, 8 - shift, 0), kept)
+            tail = jnp.concatenate([acts[:dec_rows], kept.astype(BF16)], axis=0)
             fin[m] = rms_norm(tail, g_final[...].astype(F32)[None, :])
-            for target in range(n_stages - 1):
+            for target in fin_first:
                 fin_send(m, target).start()
+
+        if loading:
+            send_rows()
+        else:
+            pl.when(stage < last)(send_rows)
+            pl.when(stage == last)(send_final)
         return carry
 
-    lax.fori_loop(0, n_micro, tick, 0)
+    @pl.when(stage == 0)
+    def _():
+        lax.fori_loop(0, n_micro, functools.partial(tick, True), 0)
+
+    @pl.when(stage > 0)
+    def _():
+        for copy in qkv_copies + pre_copies + wo_copies + up_copies[0] + up_copies[1] + down_copies:
+            copy.wait()
+        for m in range(n_micro):
+            k_copy(m).wait()
+            v_copy(m).wait()
+        lax.fori_loop(0, n_micro, functools.partial(tick, False), 0)
+
+    for copy in head_copies:
+        copy.start()
 
     pre_out = (pltpu.make_async_copy(kp, kp_out, o_sem.at[0]), pltpu.make_async_copy(vp, vp_out, o_sem.at[1]))
     for copy in pre_out:
@@ -352,13 +372,29 @@
     def _():
         for m in range(n_micro):
             x_send(m).wait_send()
+
+    def fin_next(m):
+        return pltpu.make_async_remote_copy(
+            src_ref=fin.at[m], dst_ref=fin.at[m], send_sem=fnext_sem.at[m], recv_sem=frecv_sem.at[m],
+            device_id={'stage': jnp.maximum(stage - 1, 0)}, device_id_type=MESH)
+
+    @pl.when(passes_on)
+    def _():
         for m in range(n_micro):
-            fin_send(m, 0).wait_recv()
+            fin_next(m).wait_recv()
+            fin_next(m).start()
+        for m in range(n_micro):
+            fin_next(m).wait_send()
+
+    @pl.when((stage < last) & jnp.logical_not(passes_on))
+    def _():
+        for m in range(n_micro):
+            fin_next(m).wait_recv()
 
     @pl.when(stage == last)
     def _():
         for m in range(n_micro):
-            for target in range(n_stages - 1):
+            for target in fin_first:
                 fin_send(m, target).wait_send()
 
     fin_copy = pltpu.make_async_copy(fin, fin_out, o_sem.at[2])
@@ -389,7 +425,7 @@
     for m in range(micros):
         kept = fin[m // join].astype(F32)
         first = (m % join) * (n_kept - 1)
-        last = (n_kept - 1) * join + 8 * (m % join) + 7
+        last = fin.shape[1] - join + m % join
         for t in range(rows.shape[0]):
             tile = kept[:, t * 128:(t + 1) * 128]
             rows[t, pl.ds(m, n_kept - 1, stride=micros), :] = tile[first:first + n_kept - 1]
@@ -440,7 +476,7 @@
         q_width = w_q.shape[2]
         ffn = w_gate.shape[2]
         vocab = w_head.shape[1]
-        fin_rows = dec_rows + 8 * JOIN
+        fin_rows = dec_rows + 8
 
         kd = jnp.transpose(k_dec[0], (0, 1, 3, 4, 2)).reshape(n_micro, dec_rows, kv_width, cache_len)
         vd = jnp.transpose(v_dec[0], (0, 1, 3, 4, 2)).reshape(n_micro, dec_rows, kv_width, cache_len)
@@ -495,6 +531,7 @@
                 pltpu.SemaphoreType.DMA((n_micro,)),
                 pltpu.SemaphoreType.DMA((n_micro, n_stages - 1)),
                 pltpu.SemaphoreType.DMA((n_micro,)),
+                pltpu.SemaphoreType.DMA((n_micro,)),
             ],
             compiler_params=pltpu.CompilerParams(collective_id=0, has_side_effects=True, vmem_limit_bytes=int(R1_MB * 1024 * 1024)),
             name='pipeline',
@@ -502,7 +539,7 @@
               inv_freq, g_attn, g_mlp, g_final, x_dec, x_pre, w_q[0], w_k[0], w_v[0], w_o[0], w_gate[0], w_up[0], w_down[0], kd, vd, kpre, vpre, w_head)))
 
         v_blk = 512
-        n_slot = 4
+        n_slot = -(-ffn // v_blk) - (ffn - vocab) // v_blk
         logits, kd_out, vd_out, kp_out, vp_out = pl.pallas_call(
             functools.partial(output_kernel, micros, vocab),
             out_shape=(
@@ -525,7 +562,7 @@
                 pltpu.SemaphoreType.DMA((4,)),
                 pltpu.SemaphoreType.DMA((n_slot,)),
             ],
-            compiler_params=pltpu.CompilerParams(vmem_limit_bytes=13 * 1024 * 1024),
+            compiler_params=pltpu.CompilerParams(vmem_limit_bytes=14 * 1024 * 1024),
             name='output',
         )(kc, vc, w1, pltpu.with_memory_space_constraint(w_head, pltpu.HBM), fin, kp, vp)
 

time: 134 us -> 125 us (0.933)
  Pallas kernels: 131 us -> 123 us
    pallas_call x1, Pallas kernels: 118 us -> 113 us  [device_fn(): pl.pallas_call(functools.partial(pipeline_kernel, n_stages), out_shape=(V...]
    pallas_call x1, Pallas kernels: 12.9 us -> 9.56 us  [device_fn(): pl.pallas_call(functools.partial(output_kernel, micros, vocab), out_shape...]
where the time goes in v4:
time: 125 us
  Pallas kernels  123 us (98%)
  between operations  1.48 us (1%)
    pallas_call x1, Pallas kernels, device_fn(): pl.pallas_call(functools.partial(pipeline_kernel, n_stages), out_shape=(V...  113 us
    pallas_call x1, Pallas kernels, device_fn(): pl.pallas_call(functools.partial(output_kernel, micros, vocab), out_shape...  9.56 us

profile of v4, /device:TPU:113, one launch (start us, length us, event | category | flops | bytes accessed | tf_op | source)
XLA Modules:
  0.0 124.8 jit_solution(13122517649683205480)
XLA Ops:
  1.3 0.0 copy-start
  1.3 0.7 copy-done
  2.0 113.1 %pipeline.1 = (bf16[2,64,128,256]{3,2,1,0:T(8,128)(2,1)S(1)}, bf16[2,64,128,256]{3,2,1,0:T(8,128)(2,1)S(1)}, bf16[896,4864]{1,0:T(8,128)(2,1)S(1)}, bf16[2,72,89...) custom-call(s32[4,32]{1,0:T(4,128)S(1)} %copy-done, s32[1]{0:T(128)S(6)} %copy.25.pre_len, ...), custom_call_target="tpu_custom_call" | custom-call | tf_op jit(solution)/shard_map/pipeline/pallas_call | solution.py:492
  115.1 9.6 %output.1 = (f32[33,4,8192]{2,1,0:T(4,128)}, bf16[2,64,128,256]{3,2,1,0:T(8,128)(2,1)}, bf16[2,64,128,256]{3,2,1,0:T(8,128)(2,1)}, bf16[128,256]{1,0:T(8,128)(2,1)}, bf16[128,256]{1,0:T(8,128)(2,1)}) custom-call(bf16[2,64,128,256]{3,2,1,0:T(8,128)(2,1)S(1)} %get-tuple-element.16.kc, bf16[2,64,128,256]{3,2,1,0:T(8,128)(2,1)S(1)} %get-tuple-element.17.vc, ...), custom_call_target="tpu_custom_call" | custom-call | tf_op jit(solution)/shard_map/output/pallas_call | solution.py:543
Async XLA Ops:
  1.3 0.7 copy-start

commit v5 on v4

--- a/solution.py
+++ b/solution.py
@@ -17,7 +17,7 @@
 VMEM = pltpu.VMEM
 SMEM = pltpu.SMEM
 MESH = pl.DeviceIdType.MESH
-R1_MB = 26
+R1_MB = 21.5
 JOIN = 2
 
 
@@ -44,8 +44,8 @@
     n_stages,
     dec_len, pre_len, inv_freq_in, g_attn_in, g_mlp_in, g_final_in,
     x_dec, x_pre, w_q, w_k, w_v, w_o, w_gate, w_up, w_down, k_dec, v_dec, k_pre, v_pre, w_head,
-    kc, vc, w1, fin_out, kp_out, vp_out,
-    inv_freq, g_attn, g_mlp, g_final, wqkv, wo, w3, w2, kp, vp, xin, fin, qd, kn, vn, cosv, sinv, hid, sp,
+    kc, vc, w1, w3, fin_out, kp_out, vp_out,
+    inv_freq, g_attn, g_mlp, g_final, wqkv, wo, w2, kp, vp, xin, fin, qd, kn, vn, cosv, sinv, hid, sp,
     w_sem, kv_sem, p_sem, x_sem, o_sem, g_sem, send_sem, recv_sem, fsend_sem, frecv_sem, fnext_sem,
 ):
     n_micro, n_rows, hidden = xin.shape
@@ -95,8 +95,15 @@
         )
         for i in range(2)
     )
-    head_copies = (pltpu.make_async_copy(w_head.at[:, pl.ds(0, ffn)], w1, w_sem.at[9]),)
-    down_copies = (pltpu.make_async_copy(w_down, w2, w_sem.at[8]),)
+    rest = w_head.shape[1] - ffn
+    head_copies = (
+        pltpu.make_async_copy(w_head.at[:, pl.ds(0, ffn)], w1, w_sem.at[9]),
+        pltpu.make_async_copy(w_head.at[:, pl.ds(ffn, rest)], w3.at[:, pl.ds(0, rest)], w_sem.at[10]),
+    )
+    cut = ffn // 512 * 256 + 256
+    down_copies = tuple(
+        pltpu.make_async_copy(w_down.at[pl.ds(lo, size)], w2.at[pl.ds(lo, size)], w_sem.at[sem])
+        for lo, size, sem in ((0, cut, 8), (cut, ffn - cut, 11)))
 
     gain_copies = [pltpu.make_async_copy(src, dst, g_sem.at[i]) for i, (src, dst) in enumerate((
         (inv_freq_in, inv_freq), (g_attn_in, g_attn), (g_mlp_in, g_mlp), (g_final_in, g_final)))]
@@ -246,11 +253,7 @@
                 keep = low_half if j % 2 == 0 else jnp.logical_not(low_half)
                 rows.append(jnp.where(keep, q_tiles[j // 2][dec_rows:], 0.0).astype(BF16))
             k_g = kp_f[g * head_dim:(g + 1) * head_dim]
-            sp[...] = dot(jnp.concatenate(rows, axis=0), jnp.concatenate([k_g, k_g], axis=0))
-            for j in range(group):
-                scores = sp[j * seg_len:(j + 1) * seg_len, :] * scale
-                base = (g * group + j) * seg_len
-                hid[base:base + seg_len, :] = softmax(jnp.where(pre_valid, scores, NEG)).astype(BF16)
+            sp[g * span:(g + 1) * span, :] = dot(jnp.concatenate(rows, axis=0), jnp.concatenate([k_g, k_g], axis=0))
 
         if loading:
             k_copy(m).wait()
@@ -258,26 +261,29 @@
         for b in range(dec_rows):
             pos = dec_len[m * (dec_rows // per_micro) + b // per_micro, b % per_micro]
             q_b = qd[b * 16:(b + 1) * 16, :]
-            s_old = dot(q_b.astype(BF16), kc[m, b]) * scale
+            s_old = jnp.where(pos_lane < pos, dot(q_b.astype(BF16), kc[m, b]) * scale, NEG)
             s_new = jnp.sum(q_b * kn[m, b:b + 1, :], axis=-1, keepdims=True) * scale
-            here = pos_lane == pos
-            scores = jnp.where(here, s_new, jnp.where(pos_lane < pos, s_old, NEG))
-            peak = jnp.max(scores, axis=-1, keepdims=True)
-            expd = jnp.exp(scores - peak)
-            inv = 1.0 / jnp.sum(expd, axis=-1, keepdims=True)
-            hid[pd_base + b * 16:pd_base + (b + 1) * 16, :] = jnp.where(here, 0.0, expd * inv).astype(BF16)
-            p_new = (jnp.exp(s_new - peak) * inv).astype(BF16).astype(F32)
+            peak = jnp.maximum(jnp.max(s_old, axis=-1, keepdims=True), s_new)
+            expd = jnp.exp(s_old - peak)
+            e_new = jnp.exp(s_new - peak)
+            inv = 1.0 / (jnp.sum(expd, axis=-1, keepdims=True) + e_new)
+            hid[pd_base + b * 16:pd_base + (b + 1) * 16, :] = (expd * inv).astype(BF16)
+            p_new = (e_new * inv).astype(BF16).astype(F32)
             qd[b * 16:(b + 1) * 16, :] = p_new * vn[m, b:b + 1, :]
 
+        if loading:
+            v_copy(m).wait()
+        for j in range(q_heads):
+            scores = sp[j * seg_len:(j + 1) * seg_len, :] * scale
+            hid[j * seg_len:(j + 1) * seg_len, :] = softmax(jnp.where(pre_valid, scores, NEG)).astype(BF16)
+        for b in range(dec_rows):
+            qd[b * 16:(b + 1) * 16, :] += dot_t(hid[pd_base + b * 16:pd_base + (b + 1) * 16, :], vc[m, b])
         pre_heads = []
         for g in range(kv_count):
             v_g = vp_f[g * head_dim:(g + 1) * head_dim]
             mixed = dot_t(hid[g * span:(g + 1) * span, :], jnp.concatenate([v_g, v_g], axis=0))
             pre_heads += [mixed[i * seg_len:(i + 1) * seg_len] for i in range(group)]
-        if loading:
-            v_copy(m).wait()
-        for b in range(dec_rows):
-            qd[b * 16:(b + 1) * 16, :] += dot_t(hid[pd_base + b * 16:pd_base + (b + 1) * 16, :], vc[m, b])
+
 
         att_tiles = []
         for t in range(q_width // 128):
@@ -308,9 +314,17 @@
                 k = n // n_blk
                 hid[k * n_rows:(k + 1) * n_rows, :] = (jax.nn.silu(gate) * up).astype(BF16)
 
-        wait_first(down_copies)
-        hidden_act = jnp.concatenate([hid[k * n_rows:(k + 1) * n_rows, :] for k in range(ffn // n_blk)], axis=1)
-        acts = (acts.astype(F32) + dot(hidden_act, w2[...])).astype(BF16)
+        def act_blocks(lo, hi):
+            return jnp.concatenate([hid[k * n_rows:(k + 1) * n_rows, :] for k in range(lo // n_blk, hi // n_blk)], axis=1)
+
+        if loading:
+            wait_first(down_copies[:1])
+            down = dot(act_blocks(0, cut), w2[:cut, :])
+            wait_first(down_copies[1:])
+            down = down + dot(act_blocks(cut, ffn), w2[cut:, :])
+        else:
+            down = dot(act_blocks(0, ffn), w2[...])
+        acts = (acts.astype(F32) + down).astype(BF16)
 
         def send_rows():
             xin[m] = acts
@@ -406,7 +420,7 @@
         copy.wait()
 
 
-def output_kernel(micros, vocab, kc, vc, w_low, w_all, fin_in, kp_in, vp_in, logits, kc_out, vc_out, kp_out, vp_out, w_high, fin, kp, vp, rows, stage_buf, i_sem, c_sem, l_sem):
+def output_kernel(micros, vocab, kc, vc, w_low, w_high, fin_in, kp_in, vp_in, logits, kc_out, vc_out, kp_out, vp_out, fin, kp, vp, rows, stage_buf, i_sem, c_sem, l_sem):
     n_chunk = fin.shape[0]
     n_kept = logits.shape[0]
     join = micros // n_chunk
@@ -414,8 +428,7 @@
     copies = [pltpu.make_async_copy(src, dst, c_sem.at[i]) for i, (src, dst) in enumerate(((kc, kc_out), (vc, vc_out), (kp, kp_out), (vp, vp_out)))]
     loads = [pltpu.make_async_copy(src, dst, i_sem.at[i]) for i, (src, dst) in enumerate(((fin_in, fin), (kp_in, kp), (vp_in, vp)))]
     low = w_low.shape[1]
-    w_load = pltpu.make_async_copy(w_all.at[:, pl.ds(low, vocab - low)], w_high, i_sem.at[3])
-    for copy in loads + [w_load] + copies[:2]:
+    for copy in loads + copies[:2]:
         copy.start()
     for copy in loads:
         copy.wait()
@@ -443,8 +456,6 @@
     for i, (w_ref, base, n, width) in enumerate(blocks):
         if i >= n_slot:
             store(i - n_slot).wait()
-        if base and n == 0:
-            w_load.wait()
         out = dot(lhs, w_ref[:, n:n + width])
         for r in range(n_kept):
             stage_buf[i % n_slot, r, :, :width] = out[r * micros:(r + 1) * micros]
@@ -489,18 +500,19 @@
         def spec(space):
             return pl.BlockSpec(memory_space=space)
 
-        kc, vc, w1, fin, kp, vp = pl.pallas_call(
+        kc, vc, w1, w3, fin, kp, vp = pl.pallas_call(
             functools.partial(pipeline_kernel, n_stages),
             out_shape=(
                 VMEM((n_micro, dec_rows, kv_width, cache_len), BF16),
                 VMEM((n_micro, dec_rows, kv_width, cache_len), BF16),
                 VMEM((hidden, ffn), BF16),
-                jax.ShapeDtypeStruct((n_micro, fin_rows, hidden), BF16),
-                jax.ShapeDtypeStruct((kv_width, cache_len), BF16),
-                jax.ShapeDtypeStruct((kv_width, cache_len), BF16),
+                VMEM((hidden, ffn), BF16),
+                pltpu.HBM((n_micro, fin_rows, hidden), BF16),
+                pltpu.HBM((kv_width, cache_len), BF16),
+                pltpu.HBM((kv_width, cache_len), BF16),
             ),
             in_specs=[spec(SMEM)] * 2 + [spec(HBM)] * 18,
-            out_specs=(spec(VMEM),) * 3 + (spec(HBM),) * 3,
+            out_specs=(spec(VMEM),) * 4 + (spec(pltpu.HBM),) * 3,
             scratch_shapes=[
                 VMEM((1, 128), F32),
                 VMEM((1, hidden), BF16),
@@ -508,7 +520,6 @@
                 VMEM((hidden,), BF16),
                 VMEM((hidden, q_width + 2 * kv_width), BF16),
                 VMEM((q_width, hidden), BF16),
-                VMEM((hidden, ffn), BF16),
                 VMEM((ffn, hidden), BF16),
                 VMEM((kv_width, cache_len), BF16),
                 VMEM((kv_width, cache_len), BF16),
@@ -520,8 +531,8 @@
                 VMEM((n_micro, n_rows, 128), F32),
                 VMEM((n_micro, n_rows, 128), F32),
                 VMEM((ffn // 256 * n_rows, 256), BF16),
-                VMEM((q_width // head_dim // kv_count * seg_len, cache_len), F32),
-                pltpu.SemaphoreType.DMA((10,)),
+                VMEM((q_width // head_dim * seg_len, cache_len), F32),
+                pltpu.SemaphoreType.DMA((12,)),
                 pltpu.SemaphoreType.DMA((n_micro, 2)),
                 pltpu.SemaphoreType.DMA((2,)),
                 pltpu.SemaphoreType.DMA((n_micro, 2)),
@@ -549,10 +560,9 @@
                 jax.ShapeDtypeStruct(kpre.shape, BF16),
                 jax.ShapeDtypeStruct(vpre.shape, BF16),
             ),
-            in_specs=[spec(VMEM)] * 3 + [spec(HBM)] * 4,
+            in_specs=[spec(VMEM)] * 4 + [spec(HBM)] * 3,
             out_specs=(spec(HBM),) * 5,
             scratch_shapes=[
-                VMEM((hidden, vocab - ffn), BF16),
                 VMEM((n_micro, fin_rows, hidden), BF16),
                 VMEM((kv_width, cache_len), BF16),
                 VMEM((kv_width, cache_len), BF16),
@@ -562,9 +572,9 @@
                 pltpu.SemaphoreType.DMA((4,)),
                 pltpu.SemaphoreType.DMA((n_slot,)),
             ],
-            compiler_params=pltpu.CompilerParams(vmem_limit_bytes=14 * 1024 * 1024),
+            compiler_params=pltpu.CompilerParams(vmem_limit_bytes=7 * 1024 * 1024),
             name='output',
-        )(kc, vc, w1, pltpu.with_memory_space_constraint(w_head, pltpu.HBM), fin, kp, vp)
+        )(kc, vc, w1, w3, *(pltpu.with_memory_space_constraint(arr, pltpu.HBM) for arr in (fin, kp, vp)))
 
         def dec_cache(arr):
             return jnp.transpose(arr.reshape(micros, micro_rows, kv_count, head_dim, cache_len), (0, 1, 4, 2, 3))[None]

time: 125 us -> 122 us (0.976)
  Pallas kernels: 123 us -> 120 us
    pallas_call x1, Pallas kernels: 9.56 us -> 7.47 us  [device_fn(): pl.pallas_call(functools.partial(output_kernel, micros, vocab), out_shape...]
where the time goes in v5:
time: 122 us; the launch traced here: 121 us
  Pallas kernels  120 us (98%)
  between operations  1.45 us (1%)
    pallas_call x1, Pallas kernels, device_fn(): pl.pallas_call(functools.partial(pipeline_kernel, n_stages), out_shape=(V...  112 us
    pallas_call x1, Pallas kernels, device_fn(): pl.pallas_call(functools.partial(output_kernel, micros, vocab), out_shape...  7.47 us

profile of v5, /device:TPU:113, one launch (start us, length us, event | category | flops | bytes accessed | tf_op | source)
XLA Modules:
  0.0 121.4 jit_solution(1033172526552722357)
XLA Ops:
  1.3 112.5 %pipeline.1 = (bf16[2,64,128,256]{3,2,1,0:T(8,128)(2,1)S(1)}, bf16[2,64,128,256]{3,2,1,0:T(8,128)(2,1)S(1)}, bf16[896,4864]{1,0:T(8,128)(2,1)S(1)}, bf16[896,486...) custom-call(s32[4,32]{1,0:T(4,128)} %dec_len.1, ...), custom_call_target="tpu_custom_call" | custom-call | tf_op jit(solution)/shard_map/pipeline/pallas_call | solution.py:503
  113.8 7.5 %output.1 = (f32[33,4,8192]{2,1,0:T(4,128)}, bf16[2,64,128,256]{3,2,1,0:T(8,128)(2,1)}, bf16[2,64,128,256]{3,2,1,0:T(8,128)(2,1)}, bf16[128,256]{1,0:T(8,128)(2,1)}, bf16[128,256]{1,0:T(8,128)(2,1)}) custom-call(bf16[2,64,128,256]{3,2,1,0:T(8,128)(2,1)S(1)} %get-tuple-element.17.kc, bf16[2,64,128,256]{3,2,1,0:T(8,128)(2,1)S(1)} %get-tuple-element.18.vc, ...), custom_call_target="tpu_custom_call" | custom-call | tf_op jit(solution)/shard_map/output/pallas_call | solution.py:554

commit v6 on v5

--- a/solution.py
+++ b/solution.py
@@ -130,7 +130,9 @@
     def _():
         pl.semaphore_signal(barrier, inc=1, device_id={'stage': stage - 1}, device_id_type=MESH)
 
-    fin_first = [last - 1] + list(range(last - 2, 0, -2))
+    n_chips = n_stages // 2
+    hops = {t: min((last - t) // 2, n_chips - (last - t) // 2) for t in range(1, last, 2)}
+    fin_first = sorted(hops, key=lambda t: -hops[t]) + [last - 1]
     passes_on = (stage % 2 == 1) & (stage < last)
     ends_chain = (stage % 2 == 0) & (stage < last - 1)
 
@@ -191,16 +193,16 @@
     def tick(loading, m, carry):
         def wait_first(copies):
             if loading:
-                @pl.when(m == 0)
-                def _():
-                    for copy in copies:
-                        copy.wait()
+                for copy in copies:
+                    copy.wait()
 
         if loading:
             for copy in x_copies(m):
                 copy.wait()
         else:
-            x_send(m).wait_recv()
+            @pl.when(stage > 0)
+            def _():
+                x_send(m).wait_recv()
         wait_first(qkv_copies + pre_copies)
 
         acts = xin[m]
@@ -351,7 +353,10 @@
 
     @pl.when(stage == 0)
     def _():
-        lax.fori_loop(0, n_micro, functools.partial(tick, True), 0)
+        tick(True, 0, 0)
+        for m in range(1, n_micro):
+            for copy in x_copies(m) + (k_copy(m), v_copy(m)):
+                copy.wait()
 
     @pl.when(stage > 0)
     def _():
@@ -360,7 +365,8 @@
         for m in range(n_micro):
             k_copy(m).wait()
             v_copy(m).wait()
-        lax.fori_loop(0, n_micro, functools.partial(tick, False), 0)
+
+    lax.fori_loop(jnp.maximum(1 - stage, 0), n_micro, functools.partial(tick, False), 0)
 
     for copy in head_copies:
         copy.start()

time: 122 us -> 121 us (level)
  no operation moved by 1% of the time
where the time goes in v6:
time: 121 us
  Pallas kernels  119 us (98%)
  between operations  1.45 us (1%)
    pallas_call x1, Pallas kernels, device_fn(): pl.pallas_call(functools.partial(pipeline_kernel, n_stages), out_shape=(V...  112 us
    pallas_call x1, Pallas kernels, device_fn(): pl.pallas_call(functools.partial(output_kernel, micros, vocab), out_shape...  7.47 us

profile of v6, /device:TPU:113, one launch (start us, length us, event | category | flops | bytes accessed | tf_op | source)
XLA Modules:
  0.0 120.7 jit_solution(15470444648723205461)
XLA Ops:
  1.3 111.7 %pipeline.1 = (bf16[2,64,128,256]{3,2,1,0:T(8,128)(2,1)S(1)}, bf16[2,64,128,256]{3,2,1,0:T(8,128)(2,1)S(1)}, bf16[896,4864]{1,0:T(8,128)(2,1)S(1)}, bf16[896,486...) custom-call(s32[4,32]{1,0:T(4,128)} %dec_len.1, ...), custom_call_target="tpu_custom_call" | custom-call | tf_op jit(solution)/shard_map/pipeline/pallas_call | solution.py:509
  113.0 7.5 %output.1 = (f32[33,4,8192]{2,1,0:T(4,128)}, bf16[2,64,128,256]{3,2,1,0:T(8,128)(2,1)}, bf16[2,64,128,256]{3,2,1,0:T(8,128)(2,1)}, bf16[128,256]{1,0:T(8,128)(2,1)}, bf16[128,256]{1,0:T(8,128)(2,1)}) custom-call(bf16[2,64,128,256]{3,2,1,0:T(8,128)(2,1)S(1)} %get-tuple-element.17.kc, bf16[2,64,128,256]{3,2,1,0:T(8,128)(2,1)S(1)} %get-tuple-element.18.vc, ...), custom_call_target="tpu_custom_call" | custom-call | tf_op jit(solution)/shard_map/output/pallas_call | solution.py:560

commit v7 on v6

--- a/solution.py
+++ b/solution.py
@@ -114,17 +114,25 @@
     def _():
         for copy in x_copies(0):
             copy.start()
-    for copy in qkv_copies + pre_copies + (k_copy(0), v_copy(0)) + wo_copies + up_copies[0] + up_copies[1] + down_copies:
+    for copy in qkv_copies + pre_copies + (k_copy(0), v_copy(0)) + wo_copies:
         copy.start()
+    later = [up_copies[0], up_copies[1], down_copies, (k_copy(1), v_copy(1)) if n_micro > 1 else ()]
+    later[-1] += tuple(copy for m in range(2, n_micro) for copy in (k_copy(m), v_copy(m)))
+
+    def start_later(i):
+        for copy in later[i]:
+            copy.start()
 
     @pl.when(stage == 0)
     def _():
         for m in range(1, n_micro):
             for copy in x_copies(m):
                 copy.start()
-    for m in range(1, n_micro):
-        for copy in (k_copy(m), v_copy(m)):
-            copy.start()
+
+    @pl.when(stage > 0)
+    def _():
+        for i in range(len(later)):
+            start_later(i)
 
     @pl.when(stage > 0)
     def _():
@@ -204,6 +212,8 @@
             def _():
                 x_send(m).wait_recv()
         wait_first(qkv_copies + pre_copies)
+        if loading:
+            start_later(0)
 
         acts = xin[m]
         normed = rms_norm(acts, g_attn[...])
@@ -259,6 +269,7 @@
 
         if loading:
             k_copy(m).wait()
+            start_later(1)
         pos_lane = lax.broadcasted_iota(jnp.int32, (16, cache_len), 1)
         for b in range(dec_rows):
             pos = dec_len[m * (dec_rows // per_micro) + b // per_micro, b % per_micro]
@@ -275,6 +286,7 @@
 
         if loading:
             v_copy(m).wait()
+            start_later(2)
         for j in range(q_heads):
             scores = sp[j * seg_len:(j + 1) * seg_len, :] * scale
             hid[j * seg_len:(j + 1) * seg_len, :] = softmax(jnp.where(pre_valid, scores, NEG)).astype(BF16)
@@ -308,6 +320,8 @@
         n_blk = 256
         for i in range(2):
             wait_first(up_copies[i])
+            if loading and i == 1:
+                start_later(3)
             lo = 0 if i == 0 else half // n_blk * n_blk
             hi = half // n_blk * n_blk if i == 0 else ffn
             for n in range(lo, hi, n_blk):

time: 121 us -> 114 us (0.942)
  Pallas kernels: 119 us -> 112 us
    pallas_call x1, Pallas kernels: 112 us -> 105 us  [device_fn(): pl.pallas_call(functools.partial(pipeline_kernel, n_stages), out_shape=(V...]
where the time goes in v7:
time: 114 us
  Pallas kernels  112 us (98%)
  between operations  1.45 us (1%)
    pallas_call x1, Pallas kernels, device_fn(): pl.pallas_call(functools.partial(pipeline_kernel, n_stages), out_shape=(V...  105 us
    pallas_call x1, Pallas kernels, device_fn(): pl.pallas_call(functools.partial(output_kernel, micros, vocab), out_shape...  7.47 us

profile of v7, /device:TPU:113, one launch (start us, length us, event | category | flops | bytes accessed | tf_op | source)
XLA Modules:
  0.0 113.8 jit_solution(1586010583720285022)
XLA Ops:
  1.3 104.9 %pipeline.1 = (bf16[2,64,128,256]{3,2,1,0:T(8,128)(2,1)S(1)}, bf16[2,64,128,256]{3,2,1,0:T(8,128)(2,1)S(1)}, bf16[896,4864]{1,0:T(8,128)(2,1)S(1)}, bf16[896,486...) custom-call(s32[4,32]{1,0:T(4,128)} %dec_len.1, ...), custom_call_target="tpu_custom_call" | custom-call | tf_op jit(solution)/shard_map/pipeline/pallas_call | solution.py:523
  106.2 7.5 %output.1 = (f32[33,4,8192]{2,1,0:T(4,128)}, bf16[2,64,128,256]{3,2,1,0:T(8,128)(2,1)}, bf16[2,64,128,256]{3,2,1,0:T(8,128)(2,1)}, bf16[128,256]{1,0:T(8,128)(2,1)}, bf16[128,256]{1,0:T(8,128)(2,1)}) custom-call(bf16[2,64,128,256]{3,2,1,0:T(8,128)(2,1)S(1)} %get-tuple-element.17.kc, bf16[2,64,128,256]{3,2,1,0:T(8,128)(2,1)S(1)} %get-tuple-element.18.vc, ...), custom_call_target="tpu_custom_call" | custom-call | tf_op jit(solution)/shard_map/output/pallas_call | solution.py:574

commit v8 on v7

--- a/solution.py
+++ b/solution.py
@@ -114,9 +114,9 @@
     def _():
         for copy in x_copies(0):
             copy.start()
-    for copy in qkv_copies + pre_copies + (k_copy(0), v_copy(0)) + wo_copies:
+    for copy in qkv_copies + pre_copies + (k_copy(0),):
         copy.start()
-    later = [up_copies[0], up_copies[1], down_copies, (k_copy(1), v_copy(1)) if n_micro > 1 else ()]
+    later = [(v_copy(0),) + wo_copies + up_copies[0], up_copies[1], down_copies, (k_copy(1), v_copy(1)) if n_micro > 1 else ()]
     later[-1] += tuple(copy for m in range(2, n_micro) for copy in (k_copy(m), v_copy(m)))
 
     def start_later(i):

time: 114 us -> 114 us (level)
  no operation moved by 1% of the time
where the time goes in v8:
time: 114 us
  Pallas kernels  112 us (98%)
  between operations  1.45 us (1%)
    pallas_call x1, Pallas kernels, device_fn(): pl.pallas_call(functools.partial(pipeline_kernel, n_stages), out_shape=(V...  105 us
    pallas_call x1, Pallas kernels, device_fn(): pl.pallas_call(functools.partial(output_kernel, micros, vocab), out_shape...  7.47 us

profile of v8, /device:TPU:113, one launch (start us, length us, event | category | flops | bytes accessed | tf_op | source)
XLA Modules:
  0.0 113.9 jit_solution(6563869563359935156)
XLA Ops:
  1.3 105.0 %pipeline.1 = (bf16[2,64,128,256]{3,2,1,0:T(8,128)(2,1)S(1)}, bf16[2,64,128,256]{3,2,1,0:T(8,128)(2,1)S(1)}, bf16[896,4864]{1,0:T(8,128)(2,1)S(1)}, bf16[896,486...) custom-call(s32[4,32]{1,0:T(4,128)} %dec_len.1, ...), custom_call_target="tpu_custom_call" | custom-call | tf_op jit(solution)/shard_map/pipeline/pallas_call | solution.py:523
  106.3 7.5 %output.1 = (f32[33,4,8192]{2,1,0:T(4,128)}, bf16[2,64,128,256]{3,2,1,0:T(8,128)(2,1)}, bf16[2,64,128,256]{3,2,1,0:T(8,128)(2,1)}, bf16[128,256]{1,0:T(8,128)(2,1)}, bf16[128,256]{1,0:T(8,128)(2,1)}) custom-call(bf16[2,64,128,256]{3,2,1,0:T(8,128)(2,1)S(1)} %get-tuple-element.17.kc, bf16[2,64,128,256]{3,2,1,0:T(8,128)(2,1)S(1)} %get-tuple-element.18.vc, ...), custom_call_target="tpu_custom_call" | custom-call | tf_op jit(solution)/shard_map/output/pallas_call | solution.py:574
